TPU v7x, 32 devices: a whole 2x2x4 slice. The times are simulated.
32 devices in a mesh: tm: 4 (over y, x), rows: 8 (over z, core).
Axes of the slice: x: 2, y: 2, z: 4, core: 2. Of those that a mesh axis runs over, the one named last changes fastest.
Arguments:
- frames_in: bfloat16 [16, 128, 64, 128], P('tm', 'rows'), may hold values from -6 to 6
- conv_one: bfloat16 [64, 3, 3, 64], replicated, may hold values from -0.375 to 0.375
- conv_two: bfloat16 [64, 3, 3, 64], replicated, may hold values from -0.375 to 0.375
- temporal: bfloat16 [3, 64, 64], replicated, may hold values from -0.625 to 0.625
- conv_three: bfloat16 [64, 3, 3, 64], replicated, may hold values from -0.375 to 0.375
- conv_four: bfloat16 [64, 3, 3, 64], replicated, may hold values from -0.375 to 0.375
- cotangent: bfloat16 [16, 128, 64, 128], P('tm', 'rows'), may hold values from -6 to 6
Outputs:
- decoded: bfloat16 [16, 128, 64, 128], P('tm', 'rows')
- grad_in: float32 [16, 128, 64, 128], P('tm', 'rows')
All inputs are finite; a program needn't handle non-finite values.
Results may differ from a plain program's by a relative error of at most 0.013.
Values may be sent and summed in bfloat16 or wider, within the bound.
No kernel may reach another device: no remote copies, remote signals or barrier semaphores. Data moves between devices by JAX's collectives and lax.ppermute only.
A program may use at most 64 MiB of HBM per device.

v0:
```python
import functools

import jax
import jax.numpy as jnp
from jax import lax
from jax.experimental import pallas as pl
from jax.experimental.pallas import tpu as pltpu
from jax.sharding import PartitionSpec as P

SQRT_HALF = 0.7071067811865476
INV_ROOT_TAU = 0.3989422804014327
LOG2_E = 1.4426950408889634
BF16 = jnp.bfloat16
F32 = jnp.float32
VMEM = pl.BlockSpec(memory_space=pltpu.VMEM)
ANY = pl.BlockSpec(memory_space=pl.ANY)
WIDE = 4


def passed_along(value, axis, steps):
    count = lax.axis_size(axis)
    first, last = (max(0, -steps), min(count, count - steps))
    return lax.ppermute(value, axis, [(source, source + steps) for source in range(first, last)])


def call(body, ins, in_specs, outs, out_specs, scratch=(), aliases=None, flops=0, name=None):
    return pl.pallas_call(
        body,
        out_shape=outs,
        in_specs=in_specs,
        out_specs=out_specs,
        scratch_shapes=list(scratch),
        input_output_aliases=aliases or {},
        cost_estimate=pl.CostEstimate(flops=flops, transcendentals=0, bytes_accessed=1 << 20),
        compiler_params=pltpu.CompilerParams(vmem_limit_bytes=48 * 1024 * 1024),
        name=name,
    )(*ins)


def edge_masks():
    at, count = lax.axis_index("rows"), lax.axis_size("rows")
    return jnp.where(at > 0, 1.0, 0.0), jnp.where(at < count - 1, 1.0, 0.0)


def masked(value, row, halo, rows, masks):
    if row < halo:
        return value * masks[0]
    if row >= rows - halo:
        return value * masks[1]
    return value


def cdf_of(v):
    return 0.5 * lax.erf(v * SQRT_HALF) + 0.5


def slope_of(v, cdf):
    return cdf + v * jnp.exp2(v * v * (-0.5 * LOG2_E)) * INV_ROOT_TAU


def shifted(v):
    width = v.shape[-1]
    lane = lax.broadcasted_iota(jnp.int32, v.shape, v.ndim - 1)
    left = jnp.where(lane == 0, 0.0, pltpu.roll(v, 1, v.ndim - 1))
    right = jnp.where(lane == width - 1, 0.0, pltpu.roll(v, width - 1, v.ndim - 1))
    return left.astype(BF16), v.astype(BF16), right.astype(BF16)


def put(triple, f, r, v):
    for ref, part in zip(triple, shifted(v)):
        ref[f, r] = part


def window(ref, f, r):
    rows, chan, width = 4, ref.shape[-2], ref.shape[-1]
    return ref[f, r : r + rows].reshape(rows * chan, width)


def contract(weights, sources, tasks, finish):
    for at in range(0, len(tasks), WIDE):
        group = tasks[at : at + WIDE]
        rhs = jnp.concatenate(
            [jnp.concatenate([source(f, r) for f, r in group], axis=1) for source in sources], axis=0
        )
        total = jnp.dot(weights[...], rhs, preferred_element_type=F32)
        width = total.shape[1] // len(group)
        for j, (f, r) in enumerate(group):
            part = total[:, j * width : (j + 1) * width]
            finish(f, r, part.reshape(2, part.shape[0] // 2, width))


def conv(weights, triple, frames, rows, finish):
    tasks = [(f, r) for r in range(0, rows, 2) for f in frames]
    contract(weights, [functools.partial(window, ref) for ref in triple], tasks, finish)


def fill(triple, f, pieces):
    at = 0
    for ref, frame, first, rows in pieces:
        for r in range(rows):
            put(triple, f, at, ref[frame, first + r].astype(F32))
            at += 1


def toeplitz(blocks):
    zero = jnp.zeros_like(blocks[0])
    top = jnp.concatenate(list(blocks) + [zero], axis=1)
    bottom = jnp.concatenate([zero] + list(blocks), axis=1)
    return jnp.concatenate([top, bottom], axis=0).astype(BF16)


def prep_body(*refs):
    kernels, temporal = refs[:4], refs[4]
    forward, backward, mix, unmix = refs[5:]
    wide = 4 * temporal.shape[1]
    for n, ref in enumerate(kernels):
        whole = ref[...].astype(F32)
        for b in range(3):
            own = [whole[:, a, b, :] for a in range(3)]
            forward[n, :, b * wide : (b + 1) * wide] = toeplitz(own)
            back = [part.T for part in own[::-1]]
            backward[n, :, (2 - b) * wide : (3 - b) * wide] = toeplitz(back)
    lags = [temporal[j].astype(F32) for j in range(3)]
    mix[...] = toeplitz(lags)
    unmix[...] = toeplitz([lag.T for lag in lags[::-1]])


def pack_body(source, cot, last, first, sems):
    rows = source.shape[1]
    copies = [
        pltpu.make_async_copy(source.at[:, rows - 4 :], last.at[:, :4], sems.at[0]),
        pltpu.make_async_copy(cot.at[:, rows - 2 :], last.at[:, 4:], sems.at[1]),
        pltpu.make_async_copy(source.at[:, :4], first.at[:, :4], sems.at[2]),
        pltpu.make_async_copy(cot.at[:, :2], first.at[:, 4:], sems.at[3]),
    ]
    for copy in copies:
        copy.start()
    for copy in copies:
        copy.wait()


def encode_body(base, source, above, below, forward, act_two, slope_one, slope_two, *scratch):
    src, mid = scratch[:3], scratch[3:]
    masks = edge_masks()
    rows = source.shape[1]
    for f in range(2):
        fill(src, f, [(above, base + f, 0, 4), (source, base + f, 0, rows), (below, base + f, 0, 4)])

    def first(f, r, v):
        for i in range(2):
            x = v[i]
            cdf = cdf_of(x)
            put(mid, f, r + i, masked(x * cdf, r + i, 3, rows + 6, masks))
            if 2 <= r + i < rows + 4:
                slope_one[f, r + i - 2] = slope_of(x, cdf).astype(BF16)

    def second(f, r, v):
        for i in range(2):
            x = v[i]
            cdf = cdf_of(x)
            act_two[f, r + i] = masked(x * cdf, r + i, 2, rows + 4, masks).astype(BF16)
            if 2 <= r + i < rows + 2:
                slope_two[f, r + i - 2] = slope_of(x, cdf).astype(BF16)

    conv(forward.at[0], src, range(2), rows + 6, first)
    conv(forward.at[1], mid, range(2), rows + 4, second)


def emit(dst, base, buf, sems, frames, rows, step):
    def send(f, r):
        copy = pltpu.make_async_copy(
            buf.at[f, pl.ds(r, step)], dst.at[base + f, pl.ds(r, step)], sems.at[f, r // step]
        )
        copy.start()
        return copy

    return send


def decode_into(weights, triple, rows, buf, dst, base, sems):
    copies = []

    def finish(f, r, v):
        buf[f, r : r + 2] = v.astype(buf.dtype)
        if r % 4 == 2:
            copies.append(emit(dst, base, buf, sems, 2, rows, 4)(f, r - 2))

    conv(weights, triple, range(2), rows, finish)
    return copies


def middle_body(base, decode, *refs):
    refs = list(refs)
    early, late, cot, above, below, forward, backward, mix = refs[:8]
    refs = refs[8:]
    masks = edge_masks()
    rows = cot.shape[1]
    back_three, rest = refs[0], refs[1:]
    side, rest = rest[0], rest[1:]
    three, four, seed, back = rest[:3], rest[3:6], rest[6:9], rest[9:12]
    slope_three, slope_four = rest[12:14]

    def stack(f, r):
        return jnp.concatenate([early[0, r], early[1, r], late[0, r], late[1, r]], axis=0)

    def mixed(f, r, v):
        for i in range(2):
            x = v[i]
            cdf = cdf_of(x)
            put(three, i, r, x * cdf)
            if 2 <= r < rows + 2:
                slope_three[i, r - 2] = slope_of(x, cdf).astype(BF16)

    contract(mix, [stack], [(0, r) for r in range(rows + 4)], mixed)
    for f in range(2):
        fill(seed, f, [(above, base + f, 4, 2), (cot, base + f, 0, rows), (below, base + f, 4, 2)])

    def third(f, r, v):
        for i in range(2):
            x = v[i]
            cdf = cdf_of(x)
            act = masked(x * cdf, r + i, 1, rows + 2, masks)
            if decode:
                put(four, f, r + i, act)
            else:
                side[f, r + i] = act.astype(BF16)
            slope_four[f, r + i] = slope_of(x, cdf).astype(BF16)

    conv(forward.at[2], three, range(2), rows + 2, third)

    def fourth(f, r, v):
        for i in range(2):
            x = v[i] * slope_four[f, r + i].astype(F32)
            put(back, f, r + i, masked(x, r + i, 1, rows + 2, masks))

    conv(backward.at[3], seed, range(2), rows + 2, fourth)

    def fifth(f, r, v):
        for i in range(2):
            back_three[f, r + i] = (v[i] * slope_three[f, r + i].astype(F32)).astype(BF16)

    conv(backward.at[2], back, range(2), rows, fifth)
    if decode:
        buf, sems = rest[14:]
        for copy in decode_into(forward.at[3], four, rows, buf, side, base, sems):
            copy.wait()


def decode_body(base, act_four, forward, whole, out, *scratch):
    four, (buf, sems) = scratch[:3], scratch[3:]
    rows = act_four.shape[1] - 2
    for f in range(2):
        fill(four, f, [(act_four, f, 0, rows + 2)])
    for copy in decode_into(forward.at[3], four, rows, buf, out, base, sems):
        copy.wait()


def unmix_body(early, late, slope, unmix, back_two, last, first):
    rows = slope.shape[1]

    def stack(f, r):
        return jnp.concatenate([early[0, r], early[1, r], late[0, r], late[1, r]], axis=0)

    def finish(f, r, v):
        for i in range(2):
            value = (v[i] * slope[i, r].astype(F32)).astype(BF16)
            back_two[i, r] = value
            if r < 2:
                first[i, r] = value
            if r >= rows - 2:
                last[i, r - rows + 2] = value

    contract(unmix, [stack], [(0, r) for r in range(rows)], finish)


def grad_body(base, back_two, above, below, slope, backward, *refs):
    out, refs = refs[-9], refs[-8:]
    src, mid, (buf, sems) = refs[:3], refs[3:6], refs[6:]
    masks = edge_masks()
    rows = back_two.shape[1]
    for f in range(2):
        fill(src, f, [(above, f, 0, 2), (back_two, f, 0, rows), (below, f, 0, 2)])

    def first(f, r, v):
        for i in range(2):
            x = v[i] * slope[f, r + i].astype(F32)
            put(mid, f, r + i, masked(x, r + i, 1, rows + 2, masks))

    conv(backward.at[1], src, range(2), rows + 2, first)
    for copy in decode_into(backward.at[0], mid, rows, buf, out, base, sems):
        copy.wait()


def per_device(frames_in, conv_one, conv_two, temporal, conv_three, conv_four, cotangent):
    count, rows, chan, width = frames_in.shape
    unit = rows * chan * chan * width * 2 * 9 * 2

    def arr(*lead, dtype=BF16):
        return jax.ShapeDtypeStruct(tuple(lead) + (chan, width), dtype)

    def vm(*lead, dtype=BF16):
        return pltpu.VMEM(tuple(lead) + (chan, width), dtype)

    sems = pltpu.SemaphoreType.DMA((2, rows // 4))

    last, first = call(
        pack_body, (frames_in, cotangent), [ANY] * 2, [arr(count, 6)] * 2, [VMEM] * 2,
        [pltpu.SemaphoreType.DMA((4,))], name="pack",
    )
    above = passed_along(last, "rows", 1)
    below = passed_along(first, "rows", -1)
    two, four = 2 * chan, 4 * chan
    forward, backward, mix, unmix = call(
        prep_body, (conv_one, conv_two, conv_three, conv_four, temporal), [VMEM] * 5,
        [jax.ShapeDtypeStruct((4, two, 3 * four), BF16)] * 2
        + [jax.ShapeDtypeStruct((two, four), BF16)] * 2,
        [VMEM] * 4, flops=unit // 4, name="prep",
    )

    def encode(base):
        return call(
            functools.partial(encode_body, base), (frames_in, above, below, forward), [VMEM] * 4,
            [arr(2, rows + 4), arr(2, rows + 2), arr(2, rows)], [VMEM] * 3,
            [vm(2, rows + 8)] * 3 + [vm(2, rows + 6)] * 3, flops=3 * unit, name=f"encode{base}",
        )

    def middle(base, early, late, decode):
        side = arr(count, rows) if decode else arr(2, rows + 2)
        scratch = [vm(2, rows + 4)] * 3 + [vm(2, rows + 2)] * 3 + [vm(2, rows + 4)] * 3
        scratch += [vm(2, rows + 2)] * 3 + [vm(2, rows), vm(2, rows + 2)]
        if decode:
            scratch += [vm(2, rows), sems]
        return call(
            functools.partial(middle_body, base, decode),
            (early, late, cotangent, above, below, forward, backward, mix), [VMEM] * 8,
            [arr(2, rows), side], [VMEM, ANY if decode else VMEM], scratch,
            flops=5 * unit, name=f"middle{base}",
        )

    def unmixed(early, late, slope, name):
        return call(
            unmix_body, (early, late, slope, unmix), [VMEM] * 4,
            [arr(2, rows), arr(2, 2), arr(2, 2)], [VMEM] * 3, flops=unit // 3, name=name,
        )

    def grad(base, back_two, last, first, slope, whole):
        above, below = passed_along(last, "rows", 1), passed_along(first, "rows", -1)
        ins, specs = (back_two, above, below, slope, backward), [VMEM] * 5
        if whole is not None:
            ins, specs = ins + (whole,), specs + [ANY]
        return call(
            functools.partial(grad_body, base), ins, specs, arr(count, rows, dtype=F32), ANY,
            [vm(2, rows + 4)] * 3 + [vm(2, rows + 2)] * 3 + [vm(2, rows, dtype=F32), sems],
            {} if whole is None else {5: 0}, flops=2 * unit, name=f"grad{base}",
        )

    act_late, slope_one_late, slope_two_late = encode(2)
    act_before = passed_along(act_late, "tm", 1)
    act_early, slope_one_early, slope_two_early = encode(0)
    back_three_late, decoded = middle(2, act_early, act_late, True)
    back_three_early, act_four = middle(0, act_before, act_early, False)
    back_after = passed_along(back_three_early, "tm", -1)
    bt_early, last_early, first_early = unmixed(back_three_early, back_three_late, slope_two_early, "unmix0")
    decoded = call(
        functools.partial(decode_body, 0), (act_four, forward, decoded), [VMEM, VMEM, ANY],
        arr(count, rows), ANY, [vm(2, rows + 2)] * 3 + [vm(2, rows), sems], {2: 0},
        flops=unit, name="decode0",
    )
    grad_in = grad(0, bt_early, last_early, first_early, slope_one_early, None)
    bt_late, last_late, first_late = unmixed(back_three_late, back_after, slope_two_late, "unmix2")
    grad_in = grad(2, bt_late, last_late, first_late, slope_one_late, grad_in)
    return decoded, grad_in


def solution(mesh):
    split = P("tm", "rows", None, None)
    return jax.shard_map(
        per_device,
        mesh=mesh,
        in_specs=(split, P(), P(), P(), P(), P(), split),
        out_specs=(split, split),
        check_vma=False,
    )
```

profile of v0, /device:TPU:13, one launch (start us, length us, event | category | flops | bytes accessed | tf_op | source)
XLA Modules:
  0.0 66.5 jit_solution(15046337727712168386)
XLA Ops:
  0.6 0.0 copy-start
  0.6 1.2 %copy-done = bf16[4,16,64,128]{3,2,1,0:T(8,128)(2,1)S(1)} copy-done((bf16[4,16,64,128]{3,2,1,0:T(8,128)(2,1)S(1)}, bf16[4,16,64,128]{3,2,1,0:T(8,128)(2,1)}, u32[]{:S(2)}) %copy-start) | copy-done | bytes 1048600
  1.9 0.0 copy-start.2
  1.9 1.2 %copy-done.2 = bf16[4,16,64,128]{3,2,1,0:T(8,128)(2,1)S(1)} copy-done((bf16[4,16,64,128]{3,2,1,0:T(8,128)(2,1)S(1)}, bf16[4,16,64,128]{3,2,1,0:T(8,128)(2,1)}, u32[]{:S(2)}) %copy-start.2) | copy-done | bytes 1048600
  3.1 0.0 copy-start.5
  3.1 0.0 copy-start.6
  3.1 0.0 copy-start.7
  3.1 0.0 copy-start.4
  3.1 0.0 copy-start.1
  3.1 0.2 pack.1
  3.3 3.9 %collective-permute-start = (bf16[4,6,64,128]{3,2,1,0:T(8,128)(2,1)S(1)}, bf16[4,6,64,128]{3,2,1,0:T(8,128)(2,1)S(1)}, u32[]{:S(2)}, u32[]{:S(2)}) collective-permute-start(bf16[4,6,64,128]{3,2,1,0:T(8,128)(2,1)S(1)} %get-tuple-element.24), channel_id=1, source_target_pairs={{0,1},{1,2},{2,3},{3,4},{4,5},{5,6},{6,7},{8,9},{9,10},{10,11},{11... | collective-permute-start | bytes 1179656 | tf_op jit(solution)/shard_map/ppermute | solution.py:23
  7.2 1.9 %collective-permute-start.1 = (bf16[4,6,64,128]{3,2,1,0:T(8,128)(2,1)S(1)}, bf16[4,6,64,128]{3,2,1,0:T(8,128)(2,1)S(1)}, u32[]{:S(2)}, u32[]{:S(2)}) collective-permute-start(bf16[4,6,64,128]{3,2,1,0:T(8,128)(2,1)S(1)} %get-tuple-element.25), channel_id=1, source_target_pairs={{1,0},{2,1},{3,2},{4,3},{5,4},{6,5},{7,6},{9,8},{10,9},{11,10},{12... | collective-permute-start | bytes 1179656 | tf_op jit(solution)/shard_map/ppermute | solution.py:23
  9.1 0.0 copy-done.5
  9.1 0.1 copy.11.refs_0_
  9.3 0.0 copy-done.6
  9.3 0.1 copy.12.refs_1_
  9.4 0.0 copy-done.7
  9.4 0.1 copy.13.refs_2_
  9.6 0.0 copy-done.8
  9.6 0.1 copy.14.refs_3_
  9.7 0.0 copy-done.4
  9.7 1.7 %prep.1 = (bf16[4,128,768]{2,1,0:T(8,128)(2,1)S(1)}, bf16[4,128,768]{2,1,0:T(8,128)(2,1)S(1)}, bf16[128,256]{1,0:T(8,128)(2,1)S(1)}, bf16[128,256]{1,0:T(8,128)(2,1)S(1)}) custom-call(bf16[64,3,3,64]{3,2,1,0:T(4,128)(2,1)S(1)} %copy.11.refs_0_, bf16[64,3,3,64]{3,2,1,0:T(4,128)(2,1)S(1)} %copy.12.refs_1_, bf16[64,3,3,64]{3,2,1,0:T(4,128)(2,1)S(1)} %copy.13.refs_2_, ...), custom_call_target="tpu_custom_call" | custom-call | flops 75497472 | bytes 1048576 | tf_op jit(solution)/shard_map/prep/pallas_call | solution.py:27
  11.4 0.4 collective-permute-done.above.refs_3_
  11.9 4.4 %collective-permute-done.1.below.refs_4_ = bf16[4,6,64,128]{3,2,1,0:T(8,128)(2,1)S(1)} collective-permute-done((bf16[4,6,64,128]{3,2,1,0:T(8,128)(2,1)S(1)}, bf16[4,6,64,128]{3,2,1,0:T(8,128)(2,1)S(1)}, u32[]{:S(2)}, u32[]{:S(2)}) %collective-permute-start.1) | collective-permute-done | bytes 393248 | tf_op jit(solution)/shard_map/ppermute | solution.py:23
  16.3 0.0 copy-done.1
  16.3 1.8 %encode2.1 = (bf16[2,20,64,128]{3,2,1,0:T(8,128)(2,1)S(1)}, bf16[2,18,64,128]{3,2,1,0:T(8,128)(2,1)S(1)}, bf16[2,16,64,128]{3,2,1,0:T(8,128)(2,1)S(1)}) custom-call(bf16[4,16,64,128]{3,2,1,0:T(8,128)(2,1)S(1)} %copy-done.1, bf16[4,6,64,128]{3,2,1,0:T(8,128)(2,1)S(1)} %collective-permute-done.above.refs_3_, ...), custom_call_target="tpu_custom_call" | custom-call | flops 905969664 | bytes 1048576 | tf_op jit(solution)/shard_map/encode2/pallas_call | solution.py:27
  18.1 0.0 copy-start.3
  18.2 3.3 %collective-permute-start.2 = (bf16[2,20,64,128]{3,2,1,0:T(8,128)(2,1)S(1)}, bf16[2,20,64,128]{3,2,1,0:T(8,128)(2,1)S(1)}, u32[]{:S(2)}, u32[]{:S(2)}) collective-permute-start(bf16[2,20,64,128]{3,2,1,0:T(8,128)(2,1)S(1)} %get-tuple-element.27.refs_1_), channel_id=1, source_target_pairs={{0,8},{8,16},{16,24},{1,9},{9,17},{17,25},{2,10},{10,18},{18,26},{... | collective-permute-start | bytes 1966088 | tf_op jit(solution)/shard_map/ppermute | solution.py:23
  21.4 1.9 %encode0.1 = (bf16[2,20,64,128]{3,2,1,0:T(8,128)(2,1)S(1)}, bf16[2,18,64,128]{3,2,1,0:T(8,128)(2,1)S(1)}, bf16[2,16,64,128]{3,2,1,0:T(8,128)(2,1)S(1)}) custom-call(bf16[4,16,64,128]{3,2,1,0:T(8,128)(2,1)S(1)} %copy-done.1, bf16[4,6,64,128]{3,2,1,0:T(8,128)(2,1)S(1)} %collective-permute-done.above.refs_3_, ...), custom_call_target="tpu_custom_call" | custom-call | flops 905969664 | bytes 1048576 | tf_op jit(solution)/shard_map/encode0/pallas_call | solution.py:27
  23.3 13.4 %collective-permute-done.2.refs_0_ = bf16[2,20,64,128]{3,2,1,0:T(8,128)(2,1)S(1)} collective-permute-done((bf16[2,20,64,128]{3,2,1,0:T(8,128)(2,1)S(1)}, bf16[2,20,64,128]{3,2,1,0:T(8,128)(2,1)S(1)}, u32[]{:S(2)}, u32[]{:S(2)}) %collective-permute-start.2) | collective-permute-done | bytes 655392 | tf_op jit(solution)/shard_map/ppermute | solution.py:23
  36.7 0.0 copy-done.3
  36.7 2.4 %middle0.1 = (bf16[2,16,64,128]{3,2,1,0:T(8,128)(2,1)S(1)}, bf16[2,18,64,128]{3,2,1,0:T(8,128)(2,1)S(1)}) custom-call(bf16[2,20,64,128]{3,2,1,0:T(8,128)(2,1)S(1)} %collective-permute-done.2.refs_0_, bf16[2,20,64,128]{3,2,1,0:T(8,128)(2,1)S(1)} %get-tuple-element.28.refs_1_.refs_0_, bf16[4,16,64,128]{3,2,1,0:T(8,128)(2,1)S(1)} %copy-done.3, ...), custom_call_target="tpu_custom_call" | custom-call | flops 1509949440 | bytes 1048576 | tf_op jit(solution)/shard_map/middle0/pallas_call | solution.py:27
  39.1 2.3 %collective-permute-start.3 = (bf16[2,16,64,128]{3,2,1,0:T(8,128)(2,1)S(1)}, bf16[2,16,64,128]{3,2,1,0:T(8,128)(2,1)S(1)}, u32[]{:S(2)}, u32[]{:S(2)}) collective-permute-start(bf16[2,16,64,128]{3,2,1,0:T(8,128)(2,1)S(1)} %get-tuple-element.34.early), channel_id=1, source_target_pairs={{8,0},{16,8},{24,16},{9,1},{17,9},{25,17},{10,2},{18,10},{26,18},{... | collective-permute-start | bytes 1572872 | tf_op jit(solution)/shard_map/ppermute | solution.py:23
  41.4 3.8 %middle2.1 = (bf16[2,16,64,128]{3,2,1,0:T(8,128)(2,1)S(1)}, bf16[4,16,64,128]{3,2,1,0:T(8,128)(2,1)}) custom-call(bf16[2,20,64,128]{3,2,1,0:T(8,128)(2,1)S(1)} %get-tuple-element.28.refs_1_.refs_0_, bf16[2,20,64,128]{3,2,1,0:T(8,128)(2,1)S(1)} %get-tuple-element.27.refs_1_, bf16[4,16,64,128]{3,2,1,0:T(8,128)(2,1)S(1)} %copy-done.3, ...), custom_call_target="tpu_custom_call" | custom-call | flops 1509949440 | bytes 1048576 | tf_op jit(solution)/shard_map/middle2/pallas_call | solution.py:27
  45.2 0.3 unmix0.1
  45.6 3.2 %collective-permute-start.6 = (bf16[2,2,64,128]{3,2,1,0:T(8,128)(2,1)S(1)}, bf16[2,2,64,128]{3,2,1,0:T(8,128)(2,1)S(1)}, u32[]{:S(2)}, u32[]{:S(2)}) collective-permute-start(bf16[2,2,64,128]{3,2,1,0:T(8,128)(2,1)S(1)} %get-tuple-element.43), channel_id=1, source_target_pairs={{0,1},{1,2},{2,3},{3,4},{4,5},{5,6},{6,7},{8,9},{9,10},{10,11},{11... | collective-permute-start | bytes 196616 | tf_op jit(solution)/shard_map/ppermute | solution.py:23
  48.8 1.9 %collective-permute-start.7 = (bf16[2,2,64,128]{3,2,1,0:T(8,128)(2,1)S(1)}, bf16[2,2,64,128]{3,2,1,0:T(8,128)(2,1)S(1)}, u32[]{:S(2)}, u32[]{:S(2)}) collective-permute-start(bf16[2,2,64,128]{3,2,1,0:T(8,128)(2,1)S(1)} %get-tuple-element.44), channel_id=1, source_target_pairs={{1,0},{2,1},{3,2},{4,3},{5,4},{6,5},{7,6},{9,8},{10,9},{11,10},{12... | collective-permute-start | bytes 196616 | tf_op jit(solution)/shard_map/ppermute | solution.py:23
  50.7 4.0 %collective-permute-done.3.late = bf16[2,16,64,128]{3,2,1,0:T(8,128)(2,1)S(1)} collective-permute-done((bf16[2,16,64,128]{3,2,1,0:T(8,128)(2,1)S(1)}, bf16[2,16,64,128]{3,2,1,0:T(8,128)(2,1)S(1)}, u32[]{:S(2)}, u32[]{:S(2)}) %collective-permute-start.3) | collective-permute-done | bytes 524320 | tf_op jit(solution)/shard_map/ppermute | solution.py:23
  54.7 0.3 unmix2.1
  55.0 3.8 %collective-permute-start.4 = (bf16[2,2,64,128]{3,2,1,0:T(8,128)(2,1)S(1)}, bf16[2,2,64,128]{3,2,1,0:T(8,128)(2,1)S(1)}, u32[]{:S(2)}, u32[]{:S(2)}) collective-permute-start(bf16[2,2,64,128]{3,2,1,0:T(8,128)(2,1)S(1)} %get-tuple-element.38), channel_id=1, source_target_pairs={{0,1},{1,2},{2,3},{3,4},{4,5},{5,6},{6,7},{8,9},{9,10},{10,11},{11... | collective-permute-start | bytes 196616 | tf_op jit(solution)/shard_map/ppermute | solution.py:23
  58.8 1.9 %collective-permute-start.5 = (bf16[2,2,64,128]{3,2,1,0:T(8,128)(2,1)S(1)}, bf16[2,2,64,128]{3,2,1,0:T(8,128)(2,1)S(1)}, u32[]{:S(2)}, u32[]{:S(2)}) collective-permute-start(bf16[2,2,64,128]{3,2,1,0:T(8,128)(2,1)S(1)} %get-tuple-element.39), channel_id=1, source_target_pairs={{1,0},{2,1},{3,2},{4,3},{5,4},{6,5},{7,6},{9,8},{10,9},{11,10},{12... | collective-permute-start | bytes 196616 | tf_op jit(solution)/shard_map/ppermute | solution.py:23
  60.7 1.4 %decode0.1 = bf16[4,16,64,128]{3,2,1,0:T(8,128)(2,1)} custom-call(bf16[2,18,64,128]{3,2,1,0:T(8,128)(2,1)S(1)} %get-tuple-element.31.act_four, bf16[4,128,768]{2,1,0:T(8,128)(2,1)S(1)} %get-tuple-element.26.forward.refs_5_, bf16[4,16,64,128]{3,2,1,0:T(8,128)(2,1)} %get-tuple-element.32.whole), custom_call_target="tpu_custom_call", output_to_operand_aliasing={{}: (2, {})} | custom-call | flops 301989888 | bytes 1048576 | tf_op jit(solution)/shard_map/decode0/pallas_call | solution.py:27
  62.1 0.0 collective-permute-done.6.above
  62.1 0.0 collective-permute-done.7.below
  62.1 2.0 %grad0.1.refs_0_ = f32[4,16,64,128]{3,2,1,0:T(8,128)} custom-call(bf16[2,16,64,128]{3,2,1,0:T(8,128)(2,1)S(1)} %get-tuple-element.42.back_two, bf16[2,2,64,128]{3,2,1,0:T(8,128)(2,1)S(1)} %collective-permute-done.6.above, bf16[2,2,64,128]{3,2,1,0:T(8,128)(2,1)S(1)} %collective-permute-done.7.below, bf16[2,18,64,128]{3,2,1,0:T(8,128)(2,1)S(1)} %get-tuple-element.45.slope, ...), custom_call_target="tpu_custom_call" | custom-call | flops 603979776 | bytes 1048576 | tf_op jit(solution)/shard_map/grad0/pallas_call | solution.py:27
  64.2 0.0 collective-permute-done.4.above
  64.2 0.1 collective-permute-done.5.below
  64.3 2.0 %grad2.1 = f32[4,16,64,128]{3,2,1,0:T(8,128)} custom-call(bf16[2,16,64,128]{3,2,1,0:T(8,128)(2,1)S(1)} %get-tuple-element.37.back_two, bf16[2,2,64,128]{3,2,1,0:T(8,128)(2,1)S(1)} %collective-permute-done.4.above, bf16[2,2,64,128]{3,2,1,0:T(8,128)(2,1)S(1)} %collective-permute-done.5.below, ...), custom_call_target="tpu_custom_call", output_to_operand_aliasing={{}: (5, {})} | custom-call | flops 603979776 | bytes 1048576 | tf_op jit(solution)/shard_map/grad2/pallas_call | solution.py:27
  (1 shorter events, 0.0 us)
Async XLA Ops:
  0.6 1.2 %copy-start = (bf16[4,16,64,128]{3,2,1,0:T(8,128)(2,1)S(1)}, bf16[4,16,64,128]{3,2,1,0:T(8,128)(2,1)}, u32[]{:S(2)}) copy-start(bf16[4,16,64,128]{3,2,1,0:T(8,128)(2,1)} %source.5) | copy-start | bytes 3145732
  1.9 1.2 %copy-start.2 = (bf16[4,16,64,128]{3,2,1,0:T(8,128)(2,1)S(1)}, bf16[4,16,64,128]{3,2,1,0:T(8,128)(2,1)}, u32[]{:S(2)}) copy-start(bf16[4,16,64,128]{3,2,1,0:T(8,128)(2,1)} %refs_2_.4) | copy-start | bytes 3145732
  3.1 6.0 %copy-start.5 = (bf16[64,3,3,64]{3,0,2,1:T(8,128)(2,1)S(1)}, bf16[64,3,3,64]{3,0,2,1:T(8,128)(2,1)}, u32[]{:S(2)}) copy-start(bf16[64,3,3,64]{3,0,2,1:T(8,128)(2,1)} %param.8) | copy-start | bytes 221188
  3.1 6.2 %copy-start.6 = (bf16[64,3,3,64]{3,0,2,1:T(8,128)(2,1)S(1)}, bf16[64,3,3,64]{3,0,2,1:T(8,128)(2,1)}, u32[]{:S(2)}) copy-start(bf16[64,3,3,64]{3,0,2,1:T(8,128)(2,1)} %param.9) | copy-start | bytes 221188
  3.1 6.3 %copy-start.7 = (bf16[64,3,3,64]{3,0,2,1:T(8,128)(2,1)S(1)}, bf16[64,3,3,64]{3,0,2,1:T(8,128)(2,1)}, u32[]{:S(2)}) copy-start(bf16[64,3,3,64]{3,0,2,1:T(8,128)(2,1)} %param.11) | copy-start | bytes 221188
  3.1 6.5 %copy-start.8 = (bf16[64,3,3,64]{3,0,2,1:T(8,128)(2,1)S(1)}, bf16[64,3,3,64]{3,0,2,1:T(8,128)(2,1)}, u32[]{:S(2)}) copy-start(bf16[64,3,3,64]{3,0,2,1:T(8,128)(2,1)} %param.12) | copy-start | bytes 221188
  3.1 6.6 %copy-start.4 = (bf16[3,64,64]{2,1,0:T(8,128)(2,1)S(1)}, bf16[3,64,64]{2,1,0:T(8,128)(2,1)}, u32[]{:S(2)}) copy-start(bf16[3,64,64]{2,1,0:T(8,128)(2,1)} %refs_4_.1) | copy-start | bytes 73732
  3.1 13.2 %copy-start.1 = (bf16[4,16,64,128]{3,2,1,0:T(8,128)(2,1)S(1)}, bf16[4,16,64,128]{3,2,1,0:T(8,128)(2,1)}, u32[]{:S(2)}) copy-start(bf16[4,16,64,128]{3,2,1,0:T(8,128)(2,1)} %source.5) | copy-start | bytes 3145732
  3.3 8.6 %collective-permute-start = (bf16[4,6,64,128]{3,2,1,0:T(8,128)(2,1)S(1)}, bf16[4,6,64,128]{3,2,1,0:T(8,128)(2,1)S(1)}, u32[]{:S(2)}, u32[]{:S(2)}) collective-permute-start(bf16[4,6,64,128]{3,2,1,0:T(8,128)(2,1)S(1)} %get-tuple-element.24), channel_id=1, source_target_pairs={{0,1},{1,2},{2,3},{3,4},{4,5},{5,6},{6,7},{8,9},{9,10},{10,11},{11... | collective-permute-start | bytes 1179656 | tf_op jit(solution)/shard_map/ppermute | solution.py:23
  7.2 9.1 %collective-permute-start.1 = (bf16[4,6,64,128]{3,2,1,0:T(8,128)(2,1)S(1)}, bf16[4,6,64,128]{3,2,1,0:T(8,128)(2,1)S(1)}, u32[]{:S(2)}, u32[]{:S(2)}) collective-permute-start(bf16[4,6,64,128]{3,2,1,0:T(8,128)(2,1)S(1)} %get-tuple-element.25), channel_id=1, source_target_pairs={{1,0},{2,1},{3,2},{4,3},{5,4},{6,5},{7,6},{9,8},{10,9},{11,10},{12... | collective-permute-start | bytes 1179656 | tf_op jit(solution)/shard_map/ppermute | solution.py:23
  18.1 18.5 %copy-start.3 = (bf16[4,16,64,128]{3,2,1,0:T(8,128)(2,1)S(1)}, bf16[4,16,64,128]{3,2,1,0:T(8,128)(2,1)}, u32[]{:S(2)}) copy-start(bf16[4,16,64,128]{3,2,1,0:T(8,128)(2,1)} %refs_2_.4) | copy-start | bytes 3145732
  18.2 18.5 %collective-permute-start.2 = (bf16[2,20,64,128]{3,2,1,0:T(8,128)(2,1)S(1)}, bf16[2,20,64,128]{3,2,1,0:T(8,128)(2,1)S(1)}, u32[]{:S(2)}, u32[]{:S(2)}) collective-permute-start(bf16[2,20,64,128]{3,2,1,0:T(8,128)(2,1)S(1)} %get-tuple-element.27.refs_1_), channel_id=1, source_target_pairs={{0,8},{8,16},{16,24},{1,9},{9,17},{17,25},{2,10},{10,18},{18,26},{... | collective-permute-start | bytes 1966088 | tf_op jit(solution)/shard_map/ppermute | solution.py:23
  39.1 15.6 %collective-permute-start.3 = (bf16[2,16,64,128]{3,2,1,0:T(8,128)(2,1)S(1)}, bf16[2,16,64,128]{3,2,1,0:T(8,128)(2,1)S(1)}, u32[]{:S(2)}, u32[]{:S(2)}) collective-permute-start(bf16[2,16,64,128]{3,2,1,0:T(8,128)(2,1)S(1)} %get-tuple-element.34.early), channel_id=1, source_target_pairs={{8,0},{16,8},{24,16},{9,1},{17,9},{25,17},{10,2},{18,10},{26,18},{... | collective-permute-start | bytes 1572872 | tf_op jit(solution)/shard_map/ppermute | solution.py:23
  45.6 16.6 %collective-permute-start.6 = (bf16[2,2,64,128]{3,2,1,0:T(8,128)(2,1)S(1)}, bf16[2,2,64,128]{3,2,1,0:T(8,128)(2,1)S(1)}, u32[]{:S(2)}, u32[]{:S(2)}) collective-permute-start(bf16[2,2,64,128]{3,2,1,0:T(8,128)(2,1)S(1)} %get-tuple-element.43), channel_id=1, source_target_pairs={{0,1},{1,2},{2,3},{3,4},{4,5},{5,6},{6,7},{8,9},{9,10},{10,11},{11... | collective-permute-start | bytes 196616 | tf_op jit(solution)/shard_map/ppermute | solution.py:23
  48.8 13.4 %collective-permute-start.7 = (bf16[2,2,64,128]{3,2,1,0:T(8,128)(2,1)S(1)}, bf16[2,2,64,128]{3,2,1,0:T(8,128)(2,1)S(1)}, u32[]{:S(2)}, u32[]{:S(2)}) collective-permute-start(bf16[2,2,64,128]{3,2,1,0:T(8,128)(2,1)S(1)} %get-tuple-element.44), channel_id=1, source_target_pairs={{1,0},{2,1},{3,2},{4,3},{5,4},{6,5},{7,6},{9,8},{10,9},{11,10},{12... | collective-permute-start | bytes 196616 | tf_op jit(solution)/shard_map/ppermute | solution.py:23
  55.0 9.2 %collective-permute-start.4 = (bf16[2,2,64,128]{3,2,1,0:T(8,128)(2,1)S(1)}, bf16[2,2,64,128]{3,2,1,0:T(8,128)(2,1)S(1)}, u32[]{:S(2)}, u32[]{:S(2)}) collective-permute-start(bf16[2,2,64,128]{3,2,1,0:T(8,128)(2,1)S(1)} %get-tuple-element.38), channel_id=1, source_target_pairs={{0,1},{1,2},{2,3},{3,4},{4,5},{5,6},{6,7},{8,9},{9,10},{10,11},{11... | collective-permute-start | bytes 196616 | tf_op jit(solution)/shard_map/ppermute | solution.py:23
  58.8 5.6 %collective-permute-start.5 = (bf16[2,2,64,128]{3,2,1,0:T(8,128)(2,1)S(1)}, bf16[2,2,64,128]{3,2,1,0:T(8,128)(2,1)S(1)}, u32[]{:S(2)}, u32[]{:S(2)}) collective-permute-start(bf16[2,2,64,128]{3,2,1,0:T(8,128)(2,1)S(1)} %get-tuple-element.39), channel_id=1, source_target_pairs={{1,0},{2,1},{3,2},{4,3},{5,4},{6,5},{7,6},{9,8},{10,9},{11,10},{12... | collective-permute-start | bytes 196616 | tf_op jit(solution)/shard_map/ppermute | solution.py:23
where the time goes:
time: 66.9 us; the launch traced here: 66.5 us
  waiting for transfers between devices  22.3 us (33%)
  starting transfers between devices  22.2 us (33%)
  Pallas kernels  17.9 us (27%)
  local copies, waits for them, and re-layouts  2.99 us (4%)
  between operations  1.06 us (2%)
    ppermute x8, waiting for transfers between devices, passed_along(): lax.ppermute(value, axis, [(source, source + steps) for source in range(f...  22.3 us
    ppermute x8, starting transfers between devices, passed_along(): lax.ppermute(value, axis, [(source, source + steps) for source in range(f...  22.2 us
    pallas_call x11, Pallas kernels, call(): pl.pallas_call(body, out_shape=outs, in_specs=in_specs, out_specs=out_spe...  17.9 us
    unnamed x22, local copies, waits for them, and re-layouts  2.99 us
  transfers between devices with their start and end apart: 8, of which 5 were waited for; matrix products, arithmetic and copies ran while one was open for 1% of the time, Pallas kernels for 17%

commit v1 on v0

v1 whole, which is shorter than its diff:
```python
import functools

import jax
import jax.numpy as jnp
from jax import lax
from jax.experimental import pallas as pl
from jax.experimental.pallas import tpu as pltpu
from jax.sharding import PartitionSpec as P

SQRT_HALF = 0.7071067811865476
INV_ROOT_TAU = 0.3989422804014327
LOG2_E = 1.4426950408889634
BF16 = jnp.bfloat16
F32 = jnp.float32
VMEM = pl.BlockSpec(memory_space=pltpu.VMEM)
ANY = pl.BlockSpec(memory_space=pl.ANY)
HBM = pl.BlockSpec(memory_space=pltpu.HBM)
WIDE = 4


def passed_along(value, axis, steps):
    count = lax.axis_size(axis)
    return lax.ppermute(value, axis, [(source, (source + steps) % count) for source in range(count)])


def call(body, ins, in_specs, outs, out_specs, scratch=(), aliases=None, flops=0, name=None):
    return pl.pallas_call(
        body,
        out_shape=outs,
        in_specs=in_specs,
        out_specs=out_specs,
        scratch_shapes=list(scratch),
        input_output_aliases=aliases or {},
        cost_estimate=pl.CostEstimate(flops=flops, transcendentals=0, bytes_accessed=1 << 20),
        compiler_params=pltpu.CompilerParams(vmem_limit_bytes=48 * 1024 * 1024),
        name=name,
    )(*ins)


def edge_masks(axis="rows"):
    at, count = lax.axis_index(axis), lax.axis_size(axis)
    return jnp.where(at > 0, 1.0, 0.0), jnp.where(at < count - 1, 1.0, 0.0)


def tied(value, *others):
    return lax.optimization_barrier((value,) + others)[0]


def masked(value, row, halo, rows, masks):
    if row < halo:
        return value * masks[0]
    if row >= rows - halo:
        return value * masks[1]
    return value


def cdf_of(v):
    return 0.5 * lax.erf(v * SQRT_HALF) + 0.5


def slope_of(v, cdf):
    return cdf + v * jnp.exp2(v * v * (-0.5 * LOG2_E)) * INV_ROOT_TAU


def shifted(v):
    width = v.shape[-1]
    lane = lax.broadcasted_iota(jnp.int32, v.shape, v.ndim - 1)
    left = jnp.where(lane == 0, 0.0, pltpu.roll(v, 1, v.ndim - 1))
    right = jnp.where(lane == width - 1, 0.0, pltpu.roll(v, width - 1, v.ndim - 1))
    return left.astype(BF16), v.astype(BF16), right.astype(BF16)


def put(triple, f, r, v):
    for ref, part in zip(triple, shifted(v)):
        ref[f, r] = part


def window(ref, f, r):
    rows, chan, width = 4, ref.shape[-2], ref.shape[-1]
    return ref[f, r : r + rows].reshape(rows * chan, width)


def contract(weights, sources, tasks, finish):
    for at in range(0, len(tasks), WIDE):
        group = tasks[at : at + WIDE]
        rhs = jnp.concatenate(
            [jnp.concatenate([source(f, r) for f, r in group], axis=1) for source in sources], axis=0
        )
        total = jnp.dot(weights[...], rhs, preferred_element_type=F32)
        width = total.shape[1] // len(group)
        for j, (f, r) in enumerate(group):
            part = total[:, j * width : (j + 1) * width]
            finish(f, r, part.reshape(2, part.shape[0] // 2, width))


def conv(weights, triple, frames, rows, finish):
    tasks = [(f, r) for r in range(0, rows, 2) for f in range(frames)]
    contract(weights, [functools.partial(window, ref) for ref in triple], tasks, finish)


def fill(triple, f, pieces):
    at = 0
    for ref, frame, rows, mask in pieces:
        for r in range(rows):
            v = ref[frame, r].astype(F32)
            put(triple, f, at, v if mask is None else v * mask)
            at += 1


def toeplitz(blocks):
    zero = jnp.zeros_like(blocks[0])
    top = jnp.concatenate(list(blocks) + [zero], axis=1)
    bottom = jnp.concatenate([zero] + list(blocks), axis=1)
    return jnp.concatenate([top, bottom], axis=0).astype(BF16)


def prep_body(*refs):
    kernels, temporal = refs[:4], refs[4]
    forward, backward, mix, unmix = refs[5:]
    wide = 4 * temporal.shape[1]
    for n, ref in enumerate(kernels):
        whole = ref[...].astype(F32)
        for b in range(3):
            own = [whole[:, a, b, :] for a in range(3)]
            forward[n, :, b * wide : (b + 1) * wide] = toeplitz(own)
            back = [part.T for part in own[::-1]]
            backward[n, :, (2 - b) * wide : (3 - b) * wide] = toeplitz(back)
    lags = [temporal[j].astype(F32) for j in range(3)]
    mix[...] = toeplitz(lags)
    unmix[...] = toeplitz([lag.T for lag in lags[::-1]])


def pack_body(source, cot, *refs):
    sems, rows, copies = refs[-1], source.shape[1], []
    for n, (whole, edge) in enumerate(((source, 4), (cot, 2))):
        for m, at in enumerate((rows - edge, 0)):
            part = whole.at[:, pl.ds(at, edge)]
            copies.append(pltpu.make_async_copy(part, refs[2 * n + m], sems.at[2 * n + m]))
    for copy in copies:
        copy.start()
    for copy in copies:
        copy.wait()


def encode_body(base, source, above, below, forward, act_two, slope_one, slope_two, *scratch):
    src, mid = scratch[:3], scratch[3:]
    masks = edge_masks()
    frames, rows = act_two.shape[0], source.shape[1]
    for f in range(frames):
        g = base + f
        fill(src, f, [(above, g, 4, masks[0]), (source, g, rows, None), (below, g, 4, masks[1])])

    def first(f, r, v):
        for i in range(2):
            x = v[i]
            cdf = cdf_of(x)
            put(mid, f, r + i, masked(x * cdf, r + i, 3, rows + 6, masks))
            if 2 <= r + i < rows + 4:
                slope_one[f, r + i - 2] = slope_of(x, cdf).astype(BF16)

    def second(f, r, v):
        for i in range(2):
            x = v[i]
            cdf = cdf_of(x)
            act_two[f, r + i] = masked(x * cdf, r + i, 2, rows + 4, masks).astype(BF16)
            if 2 <= r + i < rows + 2:
                slope_two[f, r + i - 2] = slope_of(x, cdf).astype(BF16)

    conv(forward.at[0], src, frames, rows + 6, first)
    conv(forward.at[1], mid, frames, rows + 4, second)


def decode_into(weights, triple, frames, rows, buf, dst, base, sems):
    copies = []

    def finish(f, r, v):
        buf[f, r : r + 2] = v.astype(buf.dtype)
        if r % 4 == 2:
            at = pl.ds(r - 2, 4)
            copies.append(pltpu.make_async_copy(buf.at[f, at], dst.at[base + f, at], sems.at[f, r // 4]))
            copies[-1].start()

    conv(weights, triple, frames, rows, finish)
    return copies


def middle_body(base, outside, decode, spots, *refs):
    acts, refs = list(zip(refs, spots)), refs[len(spots) :]
    cot, above, below, forward, backward, mix = refs[:6]
    back_three, side = refs[6:8]
    three, four, seed, back = refs[8:11], refs[11:14], refs[14:17], refs[17:20]
    slope_three, slope_four = refs[20:22]
    masks = edge_masks()
    frames, rows, chan = back_three.shape[0], cot.shape[1], cot.shape[2]
    weights = mix[: frames * chan, : len(acts) * chan]
    if outside:
        known = edge_masks("tm")[0]
        cut = outside * chan
        begin = (weights[:, :cut].astype(F32) * known).astype(BF16)
        weights = jnp.concatenate([begin, weights[:, cut:]], axis=1)

    def stack(r):
        return jnp.concatenate([ref[f, r] for ref, f in acts], axis=0)

    for at in range(0, rows + 4, WIDE):
        rhs = jnp.concatenate([stack(at + j) for j in range(WIDE)], axis=1)
        total = jnp.dot(weights, rhs, preferred_element_type=F32)
        width = total.shape[1] // WIDE
        for j in range(WIDE):
            r = at + j
            for i in range(frames):
                x = total[i * chan : (i + 1) * chan, j * width : (j + 1) * width]
                cdf = cdf_of(x)
                put(three, i, r, x * cdf)
                if 2 <= r < rows + 2:
                    slope_three[i, r - 2] = slope_of(x, cdf).astype(BF16)
    for f in range(frames):
        g = base + f
        fill(seed, f, [(above, g, 2, masks[0]), (cot, g, rows, None), (below, g, 2, masks[1])])

    def third(f, r, v):
        for i in range(2):
            x = v[i]
            cdf = cdf_of(x)
            act = masked(x * cdf, r + i, 1, rows + 2, masks)
            if decode:
                put(four, f, r + i, act)
            else:
                side[f, r + i] = act.astype(BF16)
            slope_four[f, r + i] = slope_of(x, cdf).astype(BF16)

    conv(forward.at[2], three, frames, rows + 2, third)

    def fourth(f, r, v):
        for i in range(2):
            x = v[i] * slope_four[f, r + i].astype(F32)
            put(back, f, r + i, masked(x, r + i, 1, rows + 2, masks))

    conv(backward.at[3], seed, frames, rows + 2, fourth)

    def fifth(f, r, v):
        for i in range(2):
            back_three[f, r + i] = (v[i] * slope_three[f, r + i].astype(F32)).astype(BF16)

    conv(backward.at[2], back, frames, rows, fifth)
    if decode:
        buf, sems = refs[22:]
        for copy in decode_into(forward.at[3], four, frames, rows, buf, side, base, sems):
            copy.wait()


def decode_body(base, one, two, forward, whole, out, *scratch):
    four, (buf, sems) = scratch[:3], scratch[3:]
    rows = one.shape[1] - 2
    for f, ref in enumerate((one, two)):
        fill(four, f, [(ref, 0, rows + 2, None)])
    for copy in decode_into(forward.at[3], four, 2, rows, buf, out, base, sems):
        copy.wait()


def unmix_body(outside, spots, *refs):
    picked = list(zip(refs, spots))
    backs, slopes = picked[:4], picked[4:]
    unmix, back_two, last, first = refs[6:]
    rows, chan = back_two.shape[1:3]
    weights = unmix[...]
    if outside:
        known = edge_masks("tm")[1]
        cut = (4 - outside) * chan
        end = (weights[:, cut:].astype(F32) * known).astype(BF16)
        weights = jnp.concatenate([weights[:, :cut], end], axis=1)
    for at in range(0, rows, WIDE):
        rhs = jnp.concatenate(
            [jnp.concatenate([ref[f, at + j] for ref, f in backs], axis=0) for j in range(WIDE)], axis=1
        )
        total = jnp.dot(weights, rhs, preferred_element_type=F32)
        width = total.shape[1] // WIDE
        for j in range(WIDE):
            r = at + j
            for i in range(2):
                x = total[i * chan : (i + 1) * chan, j * width : (j + 1) * width]
                slope, f = slopes[i]
                value = (x * slope[f, r].astype(F32)).astype(BF16)
                back_two[i, r] = value
                if r < 2:
                    first[i, r] = value
                if r >= rows - 2:
                    last[i, r - rows + 2] = value


def grad_body(base, spots, back_two, above, below, *refs):
    slopes, backward = list(zip(refs, spots)), refs[2]
    out, refs = refs[-9], refs[-8:]
    src, mid, (buf, sems) = refs[:3], refs[3:6], refs[6:]
    masks = edge_masks()
    frames, rows = back_two.shape[:2]
    for f in range(frames):
        fill(src, f, [(above, f, 2, masks[0]), (back_two, f, rows, None), (below, f, 2, masks[1])])

    def first(f, r, v):
        for i in range(2):
            slope, g = slopes[f]
            x = v[i] * slope[g, r + i].astype(F32)
            put(mid, f, r + i, masked(x, r + i, 1, rows + 2, masks))

    conv(backward.at[1], src, frames, rows + 2, first)
    for copy in decode_into(backward.at[0], mid, frames, rows, buf, out, base, sems):
        copy.wait()


def per_device(frames_in, conv_one, conv_two, temporal, conv_three, conv_four, cotangent):
    count, rows, chan, width = frames_in.shape
    unit = rows * chan * chan * width * 2 * 9 * 2

    def arr(*lead, dtype=BF16):
        return jax.ShapeDtypeStruct(tuple(lead) + (chan, width), dtype)

    def vm(*lead, dtype=BF16):
        return pltpu.VMEM(tuple(lead) + (chan, width), dtype)

    sems = pltpu.SemaphoreType.DMA((2, rows // 4))

    last, first, cot_last, cot_first = call(
        pack_body, (frames_in, cotangent), [HBM] * 2,
        [arr(count, 4)] * 2 + [arr(count, 2)] * 2, [VMEM] * 4,
        [pltpu.SemaphoreType.DMA((4,))], name="pack",
    )
    above = passed_along(last, "rows", 1)
    below = passed_along(first, "rows", -1)
    two, four = 2 * chan, 4 * chan
    forward, backward, mix, unmix = call(
        prep_body, (conv_one, conv_two, conv_three, conv_four, temporal), [VMEM] * 5,
        [jax.ShapeDtypeStruct((4, two, 3 * four), BF16)] * 2
        + [jax.ShapeDtypeStruct((two, four), BF16)] * 2,
        [VMEM] * 4, flops=unit // 4, name="prep",
    )

    def encode(base, n):
        return call(
            functools.partial(encode_body, base), (frames_in, above, below, forward), [VMEM] * 4,
            [arr(n, rows + 4), arr(n, rows + 2), arr(n, rows)], [VMEM] * 3,
            [vm(n, rows + 8)] * 3 + [vm(n, rows + 6)] * 3, flops=3 * unit * n // 2, name=f"encode{base}",
        )

    def middle(base, n, acts, outside):
        decode = len(acts) == 4
        acts, spots = zip(*acts)
        side = arr(count, rows) if decode else arr(n, rows + 2)
        scratch = [vm(n, rows + 4)] * 3 + [vm(n, rows + 2)] * 3 + [vm(n, rows + 4)] * 3
        scratch += [vm(n, rows + 2)] * 3 + [vm(n, rows), vm(n, rows + 2)]
        if decode:
            scratch += [vm(n, rows), sems]
        return call(
            functools.partial(middle_body, base, outside, decode, spots),
            acts + (cotangent, cot_above, cot_below, forward, backward, mix),
            [VMEM] * (len(acts) + 6), [arr(n, rows), side], [VMEM, ANY if decode else VMEM], scratch,
            flops=5 * unit * n // 2, name=f"middle{base}",
        )

    def unmixed(backs, slopes, outside, name):
        ins, spots = zip(*(backs + slopes))
        return call(
            functools.partial(unmix_body, outside, spots), ins + (unmix,), [VMEM] * 7,
            [arr(2, rows), arr(2, 2), arr(2, 2)], [VMEM] * 3, flops=unit // 3, name=name,
        )

    def grad(base, back_two, above, below, slopes, whole):
        slopes, spots = zip(*slopes)
        ins, specs = (back_two, above, below) + slopes + (backward,), [VMEM] * 6
        if whole is not None:
            ins, specs = ins + (whole,), specs + [ANY]
        return call(
            functools.partial(grad_body, base, spots), ins, specs, arr(count, rows, dtype=F32), ANY,
            [vm(2, rows + 4)] * 3 + [vm(2, rows + 2)] * 3 + [vm(2, rows, dtype=F32), sems],
            {} if whole is None else {6: 0}, flops=2 * unit, name=f"grad{base}",
        )

    act_3, slope_one_3, slope_two_3 = encode(3, 1)
    before_1 = passed_along(act_3, "tm", 1)
    act_2, slope_one_2, slope_two_2 = encode(2, 1)
    before_2 = passed_along(act_2, "tm", 1)
    cot_last, cot_first, act_2 = lax.optimization_barrier((cot_last, cot_first, act_2))
    cot_above = passed_along(cot_last, "rows", 1)
    cot_below = passed_along(cot_first, "rows", -1)
    act, slope_one, slope_two = encode(0, 2)
    back_1, act_four_1 = middle(1, 1, [(before_1, 0), (act, 0), (act, 1)], 1)
    after_1 = passed_along(back_1, "tm", -1)
    before_2, back_1 = lax.optimization_barrier((before_2, back_1))
    back_0, act_four_0 = middle(0, 1, [(before_2, 0), (before_1, 0), (act, 0)], 2)
    after_0 = passed_along(back_0, "tm", -1)
    act_3, back_0 = lax.optimization_barrier((act_3, back_0))
    back_late, decoded = middle(2, 2, [(act, 0), (act, 1), (act_2, 0), (act_3, 0)], 0)
    backs = [(back_0, 0), (back_1, 0), (back_late, 0), (back_late, 1), (after_0, 0), (after_1, 0)]
    early, last, first = unmixed(backs[:4], [(slope_two, 0), (slope_two, 1)], 0, "unmix0")
    early_above, early_below = passed_along(last, "rows", 1), passed_along(first, "rows", -1)
    late, last, first = unmixed(backs[2:], [(slope_two_2, 0), (slope_two_3, 0)], 2, "unmix2")
    late_above, late_below = passed_along(last, "rows", 1), passed_along(first, "rows", -1)
    decoded = call(
        functools.partial(decode_body, 0), (act_four_0, act_four_1, forward, decoded), [VMEM] * 3 + [ANY],
        arr(count, rows), ANY, [vm(2, rows + 2)] * 3 + [vm(2, rows), sems], {3: 0},
        flops=unit, name="decode0",
    )
    grad_in = grad(0, early, early_above, early_below, [(slope_one, 0), (slope_one, 1)], None)
    grad_in = grad(2, late, late_above, late_below, [(slope_one_2, 0), (slope_one_3, 0)], grad_in)
    return decoded, grad_in


def solution(mesh):
    split = P("tm", "rows", None, None)
    return jax.shard_map(
        per_device,
        mesh=mesh,
        in_specs=(split, P(), P(), P(), P(), P(), split),
        out_specs=(split, split),
        check_vma=False,
    )
```

time: 66.9 us -> 57.3 us (0.86)
  the two profiles are of different devices: /device:TPU:13 before, /device:TPU:0 now
where the time goes in v1:
time: 57.3 us; the launch traced here: 57.1 us
  starting transfers between devices  22.8 us (40%)
  Pallas kernels  19.1 us (33%)
  waiting for transfers between devices  11.2 us (20%)
  local copies, waits for them, and re-layouts  2.99 us (5%)
  between operations  1.02 us (2%)
    ppermute x12, starting transfers between devices, passed_along(): lax.ppermute(value, axis, [(source, (source + steps) % count) for source...  22.8 us
    pallas_call x13, Pallas kernels, call(): pl.pallas_call(body, out_shape=outs, in_specs=in_specs, out_specs=out_spe...  19.1 us
    ppermute x12, waiting for transfers between devices, passed_along(): lax.ppermute(value, axis, [(source, (source + steps) % count) for source...  11.2 us
    unnamed x22, local copies, waits for them, and re-layouts  2.99 us
  transfers between devices with their start and end apart: 12, of which 5 were waited for; matrix products, arithmetic and copies ran while one was open for 1% of the time, Pallas kernels for 25%

profile of v1, /device:TPU:0, one launch (start us, length us, event | category | flops | bytes accessed | tf_op | source)
XLA Modules:
  0.0 57.1 jit_solution(11952848504546438063)
XLA Ops:
  0.6 0.0 copy-start
  0.6 1.2 %copy-done = bf16[4,16,64,128]{3,2,1,0:T(8,128)(2,1)S(1)} copy-done((bf16[4,16,64,128]{3,2,1,0:T(8,128)(2,1)S(1)}, bf16[4,16,64,128]{3,2,1,0:T(8,128)(2,1)}, u32[]{:S(2)}) %copy-start) | copy-done | bytes 1048600
  1.9 1.2 %copy-done.2 = bf16[4,16,64,128]{3,2,1,0:T(8,128)(2,1)S(1)} copy-done((bf16[4,16,64,128]{3,2,1,0:T(8,128)(2,1)S(1)}, bf16[4,16,64,128]{3,2,1,0:T(8,128)(2,1)}, u32[]{:S(2)}) %copy-start.2) | copy-done | bytes 1048600
  3.1 0.0 copy-start.4
  3.1 0.2 pack.1
  3.3 0.5 collective-permute-start
  3.8 4.1 %collective-permute-start.1 = (bf16[4,4,64,128]{3,2,1,0:T(8,128)(2,1)S(1)}, bf16[4,4,64,128]{3,2,1,0:T(8,128)(2,1)S(1)}, u32[]{:S(2)}, u32[]{:S(2)}) collective-permute-start(bf16[4,4,64,128]{3,2,1,0:T(8,128)(2,1)S(1)} %get-tuple-element.39), channel_id=1, source_target_pairs={{0,7},{1,0},{2,1},{3,2},{4,3},{5,4},{6,5},{7,6},{8,15},{9,8},{10,9... | collective-permute-start | bytes 786440 | tf_op jit(solution)/shard_map/ppermute | solution.py:23
  7.9 0.0 copy-done.5
  7.9 0.1 copy.11.refs_0_
  8.1 0.1 copy.12.refs_1_
  8.2 0.1 copy.13.refs_2_
  8.3 0.0 copy-done.8
  8.4 0.1 copy.14.refs_3_
  8.5 1.7 %prep.1 = (bf16[4,128,768]{2,1,0:T(8,128)(2,1)S(1)}, bf16[4,128,768]{2,1,0:T(8,128)(2,1)S(1)}, bf16[128,256]{1,0:T(8,128)(2,1)S(1)}, bf16[128,256]{1,0:T(8,128)(2,1)S(1)}) custom-call(bf16[64,3,3,64]{3,2,1,0:T(4,128)(2,1)S(1)} %copy.11.refs_0_, bf16[64,3,3,64]{3,2,1,0:T(4,128)(2,1)S(1)} %copy.12.refs_1_, bf16[64,3,3,64]{3,2,1,0:T(4,128)(2,1)S(1)} %copy.13.refs_2_, ...), custom_call_target="tpu_custom_call" | custom-call | flops 75497472 | bytes 1048576 | tf_op jit(solution)/shard_map/prep/pallas_call | solution.py:27
  10.2 1.9 %collective-permute-done.above = bf16[4,4,64,128]{3,2,1,0:T(8,128)(2,1)S(1)} collective-permute-done((bf16[4,4,64,128]{3,2,1,0:T(8,128)(2,1)S(1)}, bf16[4,4,64,128]{3,2,1,0:T(8,128)(2,1)S(1)}, u32[]{:S(2)}, u32[]{:S(2)}) %collective-permute-start) | collective-permute-done | bytes 262176 | tf_op jit(solution)/shard_map/ppermute | solution.py:23
  12.1 0.4 collective-permute-done.1.below
  12.6 1.1 %encode3.1 = (bf16[1,20,64,128]{3,2,1,0:T(8,128)(2,1)S(1)}, bf16[1,18,64,128]{3,2,1,0:T(8,128)(2,1)S(1)}, bf16[1,16,64,128]{3,2,1,0:T(8,128)(2,1)S(1)}) custom-call(bf16[4,16,64,128]{3,2,1,0:T(8,128)(2,1)S(1)} %copy-done.1, bf16[4,4,64,128]{3,2,1,0:T(8,128)(2,1)S(1)} %collective-permute-done.above, bf16[4,4,64,128]{3,2,1,0:T(8,128)(2,1)S(1)} %collective-permute-done.1.below, ...), custom_call_target="tpu_custom_call" | custom-call | flops 452984832 | bytes 1048576 | tf_op jit(solution)/shard_map/encode3/pallas_call | solution.py:27
  13.7 2.1 %collective-permute-start.3 = (bf16[1,20,64,128]{3,2,1,0:T(8,128)(2,1)S(1)}, bf16[1,20,64,128]{3,2,1,0:T(8,128)(2,1)S(1)}, u32[]{:S(2)}, u32[]{:S(2)}) collective-permute-start(bf16[1,20,64,128]{3,2,1,0:T(8,128)(2,1)S(1)} %get-tuple-element.56.refs_3_), channel_id=1, source_target_pairs={{0,8},{8,16},{16,24},{24,0},{1,9},{9,17},{17,25},{25,1},{2,10},{10... | collective-permute-start | bytes 983048 | tf_op jit(solution)/shard_map/ppermute | solution.py:23
  15.8 1.1 %encode2.1 = (bf16[1,20,64,128]{3,2,1,0:T(8,128)(2,1)S(1)}, bf16[1,18,64,128]{3,2,1,0:T(8,128)(2,1)S(1)}, bf16[1,16,64,128]{3,2,1,0:T(8,128)(2,1)S(1)}) custom-call(bf16[4,16,64,128]{3,2,1,0:T(8,128)(2,1)S(1)} %copy-done.1, bf16[4,4,64,128]{3,2,1,0:T(8,128)(2,1)S(1)} %collective-permute-done.above, bf16[4,4,64,128]{3,2,1,0:T(8,128)(2,1)S(1)} %collective-permute-done.1.below, ...), custom_call_target="tpu_custom_call" | custom-call | flops 452984832 | bytes 1048576 | tf_op jit(solution)/shard_map/encode2/pallas_call | solution.py:27
  16.9 0.0 copy-start.3
  17.0 1.5 %collective-permute-start.2 = (bf16[1,20,64,128]{3,2,1,0:T(8,128)(2,1)S(1)}, bf16[1,20,64,128]{3,2,1,0:T(8,128)(2,1)S(1)}, u32[]{:S(2)}, u32[]{:S(2)}) collective-permute-start(bf16[1,20,64,128]{3,2,1,0:T(8,128)(2,1)S(1)} %get-tuple-element.54.refs_2_), channel_id=1, source_target_pairs={{0,8},{8,16},{16,24},{24,0},{1,9},{9,17},{17,25},{25,1},{2,10},{10... | collective-permute-start | bytes 983048 | tf_op jit(solution)/shard_map/ppermute | solution.py:23
  18.5 1.4 %collective-permute-start.4 = (bf16[4,2,64,128]{3,2,1,0:T(8,128)(2,1)S(1)}, bf16[4,2,64,128]{3,2,1,0:T(8,128)(2,1)S(1)}, u32[]{:S(2)}, u32[]{:S(2)}) collective-permute-start(bf16[4,2,64,128]{3,2,1,0:T(8,128)(2,1)S(1)} %get-tuple-element.46), channel_id=1, source_target_pairs={{0,1},{1,2},{2,3},{3,4},{4,5},{5,6},{6,7},{7,0},{8,9},{9,10},{10,1... | collective-permute-start | bytes 393224 | tf_op jit(solution)/shard_map/ppermute | solution.py:23
  19.9 2.2 %collective-permute-start.5 = (bf16[4,2,64,128]{3,2,1,0:T(8,128)(2,1)S(1)}, bf16[4,2,64,128]{3,2,1,0:T(8,128)(2,1)S(1)}, u32[]{:S(2)}, u32[]{:S(2)}) collective-permute-start(bf16[4,2,64,128]{3,2,1,0:T(8,128)(2,1)S(1)} %get-tuple-element.47), channel_id=1, source_target_pairs={{0,7},{1,0},{2,1},{3,2},{4,3},{5,4},{6,5},{7,6},{8,15},{9,8},{10,9... | collective-permute-start | bytes 393224 | tf_op jit(solution)/shard_map/ppermute | solution.py:23
  22.0 1.8 %encode0.1 = (bf16[2,20,64,128]{3,2,1,0:T(8,128)(2,1)S(1)}, bf16[2,18,64,128]{3,2,1,0:T(8,128)(2,1)S(1)}, bf16[2,16,64,128]{3,2,1,0:T(8,128)(2,1)S(1)}) custom-call(bf16[4,16,64,128]{3,2,1,0:T(8,128)(2,1)S(1)} %copy-done.1, bf16[4,4,64,128]{3,2,1,0:T(8,128)(2,1)S(1)} %collective-permute-done.above, bf16[4,4,64,128]{3,2,1,0:T(8,128)(2,1)S(1)} %collective-permute-done.1.below, ...), custom_call_target="tpu_custom_call" | custom-call | flops 905969664 | bytes 1048576 | tf_op jit(solution)/shard_map/encode0/pallas_call | solution.py:27
  23.9 0.9 %collective-permute-done.4.refs_4_.refs_5_ = bf16[4,2,64,128]{3,2,1,0:T(8,128)(2,1)S(1)} collective-permute-done((bf16[4,2,64,128]{3,2,1,0:T(8,128)(2,1)S(1)}, bf16[4,2,64,128]{3,2,1,0:T(8,128)(2,1)S(1)}, u32[]{:S(2)}, u32[]{:S(2)}) %collective-permute-start.4) | collective-permute-done | bytes 131104 | tf_op jit(solution)/shard_map/ppermute | solution.py:23
  24.8 0.0 collective-permute-done.5.refs_5_.refs_6_
  24.8 0.0 collective-permute-done.3.refs_0_.refs_1_
  24.8 1.6 %middle1.1 = (bf16[1,16,64,128]{3,2,1,0:T(8,128)(2,1)S(1)}, bf16[1,18,64,128]{3,2,1,0:T(8,128)(2,1)S(1)}) custom-call(bf16[1,20,64,128]{3,2,1,0:T(8,128)(2,1)S(1)} %collective-permute-done.3.refs_0_.refs_1_, bf16[2,20,64,128]{3,2,1,0:T(8,128)(2,1)S(1)} %get-tuple-element.43.refs_1_.refs_2_.refs_0_, ...), custom_call_target="tpu_custom_call" | custom-call | flops 754974720 | bytes 1048576 | tf_op jit(solution)/shard_map/middle1/pallas_call | solution.py:27
  26.4 4.7 %collective-permute-done.2.refs_0_ = bf16[1,20,64,128]{3,2,1,0:T(8,128)(2,1)S(1)} collective-permute-done((bf16[1,20,64,128]{3,2,1,0:T(8,128)(2,1)S(1)}, bf16[1,20,64,128]{3,2,1,0:T(8,128)(2,1)S(1)}, u32[]{:S(2)}, u32[]{:S(2)}) %collective-permute-start.2) | collective-permute-done | bytes 327712 | tf_op jit(solution)/shard_map/ppermute | solution.py:23
  31.1 1.6 %middle0.1 = (bf16[1,16,64,128]{3,2,1,0:T(8,128)(2,1)S(1)}, bf16[1,18,64,128]{3,2,1,0:T(8,128)(2,1)S(1)}) custom-call(bf16[1,20,64,128]{3,2,1,0:T(8,128)(2,1)S(1)} %collective-permute-done.2.refs_0_, bf16[1,20,64,128]{3,2,1,0:T(8,128)(2,1)S(1)} %collective-permute-done.3.refs_0_.refs_1_, ...), custom_call_target="tpu_custom_call" | custom-call | flops 754974720 | bytes 1048576 | tf_op jit(solution)/shard_map/middle0/pallas_call | solution.py:27
  32.7 2.4 %collective-permute-start.6 = (bf16[1,16,64,128]{3,2,1,0:T(8,128)(2,1)S(1)}, bf16[1,16,64,128]{3,2,1,0:T(8,128)(2,1)S(1)}, u32[]{:S(2)}, u32[]{:S(2)}) collective-permute-start(bf16[1,16,64,128]{3,2,1,0:T(8,128)(2,1)S(1)} %get-tuple-element.67.refs_0_), channel_id=1, source_target_pairs={{0,24},{8,0},{16,8},{24,16},{1,25},{9,1},{17,9},{25,17},{2,26},{10... | collective-permute-start | bytes 786440 | tf_op jit(solution)/shard_map/ppermute | solution.py:23
  35.0 1.4 %collective-permute-start.7 = (bf16[1,16,64,128]{3,2,1,0:T(8,128)(2,1)S(1)}, bf16[1,16,64,128]{3,2,1,0:T(8,128)(2,1)S(1)}, u32[]{:S(2)}, u32[]{:S(2)}) collective-permute-start(bf16[1,16,64,128]{3,2,1,0:T(8,128)(2,1)S(1)} %get-tuple-element.68.refs_1_), channel_id=1, source_target_pairs={{0,24},{8,0},{16,8},{24,16},{1,25},{9,1},{17,9},{25,17},{2,26},{10... | collective-permute-start | bytes 786440 | tf_op jit(solution)/shard_map/ppermute | solution.py:23
  36.5 3.8 %middle2.1 = (bf16[2,16,64,128]{3,2,1,0:T(8,128)(2,1)S(1)}, bf16[4,16,64,128]{3,2,1,0:T(8,128)(2,1)}) custom-call(bf16[2,20,64,128]{3,2,1,0:T(8,128)(2,1)S(1)} %get-tuple-element.43.refs_1_.refs_2_.refs_0_, bf16[2,20,64,128]{3,2,1,0:T(8,128)(2,1)S(1)} %get-tuple-element.43.refs_1_.refs_2_.refs_0_, bf16[1,20,64,128]{3,2,1,0:T(8,128)(2,1)S(1)} %get-tuple-element.54.refs_2_, ...), custom_call_target="tpu_custom_call" | custom-call | flops 1509949440 | bytes 1048576 | tf_op jit(solution)/shard_map/middle2/pallas_call | solution.py:27
  40.3 0.3 unmix0.1
  40.6 0.3 collective-permute-start.10
  40.9 3.3 %collective-permute-start.11 = (bf16[2,2,64,128]{3,2,1,0:T(8,128)(2,1)S(1)}, bf16[2,2,64,128]{3,2,1,0:T(8,128)(2,1)S(1)}, u32[]{:S(2)}, u32[]{:S(2)}) collective-permute-start(bf16[2,2,64,128]{3,2,1,0:T(8,128)(2,1)S(1)} %get-tuple-element.72), channel_id=1, source_target_pairs={{0,7},{1,0},{2,1},{3,2},{4,3},{5,4},{6,5},{7,6},{8,15},{9,8},{10,9... | collective-permute-start | bytes 196616 | tf_op jit(solution)/shard_map/ppermute | solution.py:23
  44.2 0.0 collective-permute-done.6.refs_2_
  44.2 3.2 %collective-permute-done.7.refs_3_ = bf16[1,16,64,128]{3,2,1,0:T(8,128)(2,1)S(1)} collective-permute-done((bf16[1,16,64,128]{3,2,1,0:T(8,128)(2,1)S(1)}, bf16[1,16,64,128]{3,2,1,0:T(8,128)(2,1)S(1)}, u32[]{:S(2)}, u32[]{:S(2)}) %collective-permute-start.7) | collective-permute-done | bytes 262176 | tf_op jit(solution)/shard_map/ppermute | solution.py:23
  47.4 0.3 unmix2.1
  47.8 0.2 collective-permute-start.8
  47.9 3.4 %collective-permute-start.9 = (bf16[2,2,64,128]{3,2,1,0:T(8,128)(2,1)S(1)}, bf16[2,2,64,128]{3,2,1,0:T(8,128)(2,1)S(1)}, u32[]{:S(2)}, u32[]{:S(2)}) collective-permute-start(bf16[2,2,64,128]{3,2,1,0:T(8,128)(2,1)S(1)} %get-tuple-element.64), channel_id=1, source_target_pairs={{0,7},{1,0},{2,1},{3,2},{4,3},{5,4},{6,5},{7,6},{8,15},{9,8},{10,9... | collective-permute-start | bytes 196616 | tf_op jit(solution)/shard_map/ppermute | solution.py:23
  51.4 1.4 %decode0.1 = bf16[4,16,64,128]{3,2,1,0:T(8,128)(2,1)} custom-call(bf16[1,18,64,128]{3,2,1,0:T(8,128)(2,1)S(1)} %get-tuple-element.52.one, bf16[1,18,64,128]{3,2,1,0:T(8,128)(2,1)S(1)} %get-tuple-element.53.two, bf16[4,128,768]{2,1,0:T(8,128)(2,1)S(1)} %get-tuple-element.40.forward.refs_6_.refs_7_, ...), custom_call_target="tpu_custom_call", output_to_operand_aliasing={{}: (3, {})} | custom-call | flops 301989888 | bytes 1048576 | tf_op jit(solution)/shard_map/decode0/pallas_call | solution.py:27
  52.8 0.0 collective-permute-done.10.above
  52.8 0.0 collective-permute-done.11.below
  52.8 2.0 %grad0.1.refs_3_ = f32[4,16,64,128]{3,2,1,0:T(8,128)} custom-call(bf16[2,16,64,128]{3,2,1,0:T(8,128)(2,1)S(1)} %get-tuple-element.70.back_two, bf16[2,2,64,128]{3,2,1,0:T(8,128)(2,1)S(1)} %collective-permute-done.10.above, bf16[2,2,64,128]{3,2,1,0:T(8,128)(2,1)S(1)} %collective-permute-done.11.below, ...), custom_call_target="tpu_custom_call" | custom-call | flops 603979776 | bytes 1048576 | tf_op jit(solution)/shard_map/grad0/pallas_call | solution.py:27
  54.9 0.0 collective-permute-done.8.above
  54.9 0.0 collective-permute-done.9.below
  54.9 2.0 %grad2.1 = f32[4,16,64,128]{3,2,1,0:T(8,128)} custom-call(bf16[2,16,64,128]{3,2,1,0:T(8,128)(2,1)S(1)} %get-tuple-element.62.back_two, bf16[2,2,64,128]{3,2,1,0:T(8,128)(2,1)S(1)} %collective-permute-done.8.above, bf16[2,2,64,128]{3,2,1,0:T(8,128)(2,1)S(1)} %collective-permute-done.9.below, ...), custom_call_target="tpu_custom_call", output_to_operand_aliasing={{}: (6, {})} | custom-call | flops 603979776 | bytes 1048576 | tf_op jit(solution)/shard_map/grad2/pallas_call | solution.py:27
  (11 shorter events, 0.0 us)
Async XLA Ops:
  0.6 1.2 %copy-start = (bf16[4,16,64,128]{3,2,1,0:T(8,128)(2,1)S(1)}, bf16[4,16,64,128]{3,2,1,0:T(8,128)(2,1)}, u32[]{:S(2)}) copy-start(bf16[4,16,64,128]{3,2,1,0:T(8,128)(2,1)} %source.7) | copy-start | bytes 3145732
  1.9 1.2 %copy-start.2 = (bf16[4,16,64,128]{3,2,1,0:T(8,128)(2,1)S(1)}, bf16[4,16,64,128]{3,2,1,0:T(8,128)(2,1)}, u32[]{:S(2)}) copy-start(bf16[4,16,64,128]{3,2,1,0:T(8,128)(2,1)} %refs_4_.3) | copy-start | bytes 3145732
  3.1 4.8 %copy-start.5 = (bf16[64,3,3,64]{3,0,2,1:T(8,128)(2,1)S(1)}, bf16[64,3,3,64]{3,0,2,1:T(8,128)(2,1)}, u32[]{:S(2)}) copy-start(bf16[64,3,3,64]{3,0,2,1:T(8,128)(2,1)} %param.8) | copy-start | bytes 221188
  3.1 5.0 %copy-start.6 = (bf16[64,3,3,64]{3,0,2,1:T(8,128)(2,1)S(1)}, bf16[64,3,3,64]{3,0,2,1:T(8,128)(2,1)}, u32[]{:S(2)}) copy-start(bf16[64,3,3,64]{3,0,2,1:T(8,128)(2,1)} %param.9) | copy-start | bytes 221188
  3.1 5.1 %copy-start.7 = (bf16[64,3,3,64]{3,0,2,1:T(8,128)(2,1)S(1)}, bf16[64,3,3,64]{3,0,2,1:T(8,128)(2,1)}, u32[]{:S(2)}) copy-start(bf16[64,3,3,64]{3,0,2,1:T(8,128)(2,1)} %param.11) | copy-start | bytes 221188
  3.1 5.3 %copy-start.8 = (bf16[64,3,3,64]{3,0,2,1:T(8,128)(2,1)S(1)}, bf16[64,3,3,64]{3,0,2,1:T(8,128)(2,1)}, u32[]{:S(2)}) copy-start(bf16[64,3,3,64]{3,0,2,1:T(8,128)(2,1)} %param.12) | copy-start | bytes 221188
  3.1 5.4 %copy-start.4 = (bf16[3,64,64]{2,1,0:T(8,128)(2,1)S(1)}, bf16[3,64,64]{2,1,0:T(8,128)(2,1)}, u32[]{:S(2)}) copy-start(bf16[3,64,64]{2,1,0:T(8,128)(2,1)} %refs_4_.2) | copy-start | bytes 73732
  3.1 9.5 %copy-start.1 = (bf16[4,16,64,128]{3,2,1,0:T(8,128)(2,1)S(1)}, bf16[4,16,64,128]{3,2,1,0:T(8,128)(2,1)}, u32[]{:S(2)}) copy-start(bf16[4,16,64,128]{3,2,1,0:T(8,128)(2,1)} %source.7) | copy-start | bytes 3145732
  3.3 8.8 %collective-permute-start = (bf16[4,4,64,128]{3,2,1,0:T(8,128)(2,1)S(1)}, bf16[4,4,64,128]{3,2,1,0:T(8,128)(2,1)S(1)}, u32[]{:S(2)}, u32[]{:S(2)}) collective-permute-start(bf16[4,4,64,128]{3,2,1,0:T(8,128)(2,1)S(1)} %get-tuple-element.38), channel_id=1, source_target_pairs={{0,1},{1,2},{2,3},{3,4},{4,5},{5,6},{6,7},{7,0},{8,9},{9,10},{10,1... | collective-permute-start | bytes 786440 | tf_op jit(solution)/shard_map/ppermute | solution.py:23
  3.8 8.7 %collective-permute-start.1 = (bf16[4,4,64,128]{3,2,1,0:T(8,128)(2,1)S(1)}, bf16[4,4,64,128]{3,2,1,0:T(8,128)(2,1)S(1)}, u32[]{:S(2)}, u32[]{:S(2)}) collective-permute-start(bf16[4,4,64,128]{3,2,1,0:T(8,128)(2,1)S(1)} %get-tuple-element.39), channel_id=1, source_target_pairs={{0,7},{1,0},{2,1},{3,2},{4,3},{5,4},{6,5},{7,6},{8,15},{9,8},{10,9... | collective-permute-start | bytes 786440 | tf_op jit(solution)/shard_map/ppermute | solution.py:23
  13.7 11.1 %collective-permute-start.3 = (bf16[1,20,64,128]{3,2,1,0:T(8,128)(2,1)S(1)}, bf16[1,20,64,128]{3,2,1,0:T(8,128)(2,1)S(1)}, u32[]{:S(2)}, u32[]{:S(2)}) collective-permute-start(bf16[1,20,64,128]{3,2,1,0:T(8,128)(2,1)S(1)} %get-tuple-element.56.refs_3_), channel_id=1, source_target_pairs={{0,8},{8,16},{16,24},{24,0},{1,9},{9,17},{17,25},{25,1},{2,10},{10... | collective-permute-start | bytes 983048 | tf_op jit(solution)/shard_map/ppermute | solution.py:23
  16.9 7.9 %copy-start.3 = (bf16[4,16,64,128]{3,2,1,0:T(8,128)(2,1)S(1)}, bf16[4,16,64,128]{3,2,1,0:T(8,128)(2,1)}, u32[]{:S(2)}) copy-start(bf16[4,16,64,128]{3,2,1,0:T(8,128)(2,1)} %refs_4_.3) | copy-start | bytes 3145732
  17.0 14.2 %collective-permute-start.2 = (bf16[1,20,64,128]{3,2,1,0:T(8,128)(2,1)S(1)}, bf16[1,20,64,128]{3,2,1,0:T(8,128)(2,1)S(1)}, u32[]{:S(2)}, u32[]{:S(2)}) collective-permute-start(bf16[1,20,64,128]{3,2,1,0:T(8,128)(2,1)S(1)} %get-tuple-element.54.refs_2_), channel_id=1, source_target_pairs={{0,8},{8,16},{16,24},{24,0},{1,9},{9,17},{17,25},{25,1},{2,10},{10... | collective-permute-start | bytes 983048 | tf_op jit(solution)/shard_map/ppermute | solution.py:23
  18.5 6.3 %collective-permute-start.4 = (bf16[4,2,64,128]{3,2,1,0:T(8,128)(2,1)S(1)}, bf16[4,2,64,128]{3,2,1,0:T(8,128)(2,1)S(1)}, u32[]{:S(2)}, u32[]{:S(2)}) collective-permute-start(bf16[4,2,64,128]{3,2,1,0:T(8,128)(2,1)S(1)} %get-tuple-element.46), channel_id=1, source_target_pairs={{0,1},{1,2},{2,3},{3,4},{4,5},{5,6},{6,7},{7,0},{8,9},{9,10},{10,1... | collective-permute-start | bytes 393224 | tf_op jit(solution)/shard_map/ppermute | solution.py:23
  19.9 4.9 %collective-permute-start.5 = (bf16[4,2,64,128]{3,2,1,0:T(8,128)(2,1)S(1)}, bf16[4,2,64,128]{3,2,1,0:T(8,128)(2,1)S(1)}, u32[]{:S(2)}, u32[]{:S(2)}) collective-permute-start(bf16[4,2,64,128]{3,2,1,0:T(8,128)(2,1)S(1)} %get-tuple-element.47), channel_id=1, source_target_pairs={{0,7},{1,0},{2,1},{3,2},{4,3},{5,4},{6,5},{7,6},{8,15},{9,8},{10,9... | collective-permute-start | bytes 393224 | tf_op jit(solution)/shard_map/ppermute | solution.py:23
  32.7 11.5 %collective-permute-start.6 = (bf16[1,16,64,128]{3,2,1,0:T(8,128)(2,1)S(1)}, bf16[1,16,64,128]{3,2,1,0:T(8,128)(2,1)S(1)}, u32[]{:S(2)}, u32[]{:S(2)}) collective-permute-start(bf16[1,16,64,128]{3,2,1,0:T(8,128)(2,1)S(1)} %get-tuple-element.67.refs_0_), channel_id=1, source_target_pairs={{0,24},{8,0},{16,8},{24,16},{1,25},{9,1},{17,9},{25,17},{2,26},{10... | collective-permute-start | bytes 786440 | tf_op jit(solution)/shard_map/ppermute | solution.py:23
  35.0 12.4 %collective-permute-start.7 = (bf16[1,16,64,128]{3,2,1,0:T(8,128)(2,1)S(1)}, bf16[1,16,64,128]{3,2,1,0:T(8,128)(2,1)S(1)}, u32[]{:S(2)}, u32[]{:S(2)}) collective-permute-start(bf16[1,16,64,128]{3,2,1,0:T(8,128)(2,1)S(1)} %get-tuple-element.68.refs_1_), channel_id=1, source_target_pairs={{0,24},{8,0},{16,8},{24,16},{1,25},{9,1},{17,9},{25,17},{2,26},{10... | collective-permute-start | bytes 786440 | tf_op jit(solution)/shard_map/ppermute | solution.py:23
  40.6 12.2 %collective-permute-start.10 = (bf16[2,2,64,128]{3,2,1,0:T(8,128)(2,1)S(1)}, bf16[2,2,64,128]{3,2,1,0:T(8,128)(2,1)S(1)}, u32[]{:S(2)}, u32[]{:S(2)}) collective-permute-start(bf16[2,2,64,128]{3,2,1,0:T(8,128)(2,1)S(1)} %get-tuple-element.71), channel_id=1, source_target_pairs={{0,1},{1,2},{2,3},{3,4},{4,5},{5,6},{6,7},{7,0},{8,9},{9,10},{10,1... | collective-permute-start | bytes 196616 | tf_op jit(solution)/shard_map/ppermute | solution.py:23
  40.9 11.9 %collective-permute-start.11 = (bf16[2,2,64,128]{3,2,1,0:T(8,128)(2,1)S(1)}, bf16[2,2,64,128]{3,2,1,0:T(8,128)(2,1)S(1)}, u32[]{:S(2)}, u32[]{:S(2)}) collective-permute-start(bf16[2,2,64,128]{3,2,1,0:T(8,128)(2,1)S(1)} %get-tuple-element.72), channel_id=1, source_target_pairs={{0,7},{1,0},{2,1},{3,2},{4,3},{5,4},{6,5},{7,6},{8,15},{9,8},{10,9... | collective-permute-start | bytes 196616 | tf_op jit(solution)/shard_map/ppermute | solution.py:23
  47.8 7.1 %collective-permute-start.8 = (bf16[2,2,64,128]{3,2,1,0:T(8,128)(2,1)S(1)}, bf16[2,2,64,128]{3,2,1,0:T(8,128)(2,1)S(1)}, u32[]{:S(2)}, u32[]{:S(2)}) collective-permute-start(bf16[2,2,64,128]{3,2,1,0:T(8,128)(2,1)S(1)} %get-tuple-element.63), channel_id=1, source_target_pairs={{0,1},{1,2},{2,3},{3,4},{4,5},{5,6},{6,7},{7,0},{8,9},{9,10},{10,1... | collective-permute-start | bytes 196616 | tf_op jit(solution)/shard_map/ppermute | solution.py:23
  47.9 6.9 %collective-permute-start.9 = (bf16[2,2,64,128]{3,2,1,0:T(8,128)(2,1)S(1)}, bf16[2,2,64,128]{3,2,1,0:T(8,128)(2,1)S(1)}, u32[]{:S(2)}, u32[]{:S(2)}) collective-permute-start(bf16[2,2,64,128]{3,2,1,0:T(8,128)(2,1)S(1)} %get-tuple-element.64), channel_id=1, source_target_pairs={{0,7},{1,0},{2,1},{3,2},{4,3},{5,4},{6,5},{7,6},{8,15},{9,8},{10,9... | collective-permute-start | bytes 196616 | tf_op jit(solution)/shard_map/ppermute | solution.py:23

commit v2 on v1

--- a/solution.py
+++ b/solution.py
@@ -6,6 +6,7 @@
 from jax.experimental import pallas as pl
 from jax.experimental.pallas import tpu as pltpu
 from jax.sharding import PartitionSpec as P
+
 
 SQRT_HALF = 0.7071067811865476
 INV_ROOT_TAU = 0.3989422804014327
@@ -23,7 +24,27 @@
     return lax.ppermute(value, axis, [(source, (source + steps) % count) for source in range(count)])
 
 
-def call(body, ins, in_specs, outs, out_specs, scratch=(), aliases=None, flops=0, name=None):
+def swapped(value, first):
+    groups, count = lax.axis_size("tm"), lax.axis_size("rows")
+    pairs = []
+    for g in range(groups):
+        aside = g ^ 1 if (g ^ 1) < groups else g
+        for i in range(count):
+            j = i + 1 if (i - first) % 2 == 0 else i - 1
+            inside = 0 <= j < count
+            pairs.append((g * count + i, g * count + j if inside else aside * count + i))
+    return lax.ppermute(value, ("tm", "rows"), pairs)
+
+
+def exchanged(near, far):
+    return swapped(near, 0), swapped(far, 1)
+
+
+def is_even():
+    return lax.axis_index("rows") % 2 == 0
+
+
+def call(body, ins, in_specs, outs, out_specs, scratch=(), aliases=None, flops=0, vmem=48):
     return pl.pallas_call(
         body,
         out_shape=outs,
@@ -32,18 +53,13 @@
         scratch_shapes=list(scratch),
         input_output_aliases=aliases or {},
         cost_estimate=pl.CostEstimate(flops=flops, transcendentals=0, bytes_accessed=1 << 20),
-        compiler_params=pltpu.CompilerParams(vmem_limit_bytes=48 * 1024 * 1024),
-        name=name,
+        compiler_params=pltpu.CompilerParams(vmem_limit_bytes=vmem * 1024 * 1024),
     )(*ins)
 
 
 def edge_masks(axis="rows"):
     at, count = lax.axis_index(axis), lax.axis_size(axis)
     return jnp.where(at > 0, 1.0, 0.0), jnp.where(at < count - 1, 1.0, 0.0)
-
-
-def tied(value, *others):
-    return lax.optimization_barrier((value,) + others)[0]
 
 
 def masked(value, row, halo, rows, masks):
@@ -98,13 +114,24 @@
     contract(weights, [functools.partial(window, ref) for ref in triple], tasks, finish)
 
 
-def fill(triple, f, pieces):
-    at = 0
-    for ref, frame, rows, mask in pieces:
-        for r in range(rows):
-            v = ref[frame, r].astype(F32)
-            put(triple, f, at, v if mask is None else v * mask)
-            at += 1
+def halos(near, far, at, rows, masks):
+    even = is_even()
+
+    def side(i, mask, first, second):
+        return jnp.where(even, first[at + i].astype(F32), second[at + i].astype(F32)) * mask
+
+    above = [functools.partial(side, i, masks[0], far, near) for i in range(rows)]
+    below = [functools.partial(side, i, masks[1], near, far) for i in range(rows)]
+    return above, below
+
+
+def fill(triple, f, ref, g, rows, above=(), below=()):
+    for i, row in enumerate(above):
+        put(triple, f, i, row())
+    for r in range(rows):
+        put(triple, f, len(above) + r, ref[g, r].astype(F32))
+    for i, row in enumerate(below):
+        put(triple, f, len(above) + rows + i, row())
 
 
 def toeplitz(blocks):
@@ -119,9 +146,8 @@
     forward, backward, mix, unmix = refs[5:]
     wide = 4 * temporal.shape[1]
     for n, ref in enumerate(kernels):
-        whole = ref[...].astype(F32)
         for b in range(3):
-            own = [whole[:, a, b, :] for a in range(3)]
+            own = [ref[a, b].astype(F32) for a in range(3)]
             forward[n, :, b * wide : (b + 1) * wide] = toeplitz(own)
             back = [part.T for part in own[::-1]]
             backward[n, :, (2 - b) * wide : (3 - b) * wide] = toeplitz(back)
@@ -130,25 +156,30 @@
     unmix[...] = toeplitz([lag.T for lag in lags[::-1]])
 
 
-def pack_body(source, cot, *refs):
-    sems, rows, copies = refs[-1], source.shape[1], []
-    for n, (whole, edge) in enumerate(((source, 4), (cot, 2))):
-        for m, at in enumerate((rows - edge, 0)):
-            part = whole.at[:, pl.ds(at, edge)]
-            copies.append(pltpu.make_async_copy(part, refs[2 * n + m], sems.at[2 * n + m]))
-    for copy in copies:
-        copy.start()
-    for copy in copies:
-        copy.wait()
-
-
-def encode_body(base, source, above, below, forward, act_two, slope_one, slope_two, *scratch):
+def take(whole, g, edge, near, far, at):
+    last, even = whole.shape[1] - edge, is_even()
+    near[at : at + edge] = whole[g, pl.ds(jnp.where(even, last, 0), edge)]
+    far[at : at + edge] = whole[g, pl.ds(jnp.where(even, 0, last), edge)]
+
+
+def pack_late_body(half, source, near, far):
+    for g in range(half, source.shape[0]):
+        take(source, g, 4, near, far, 4 * (g - half))
+
+
+def pack_body(half, source, cot, near, far):
+    for g in range(half):
+        take(source, g, 4, near, far, 4 * g)
+    for g in range(source.shape[0]):
+        take(cot, g, 2, near, far, 4 * half + 2 * g)
+
+
+def encode_body(base, at, source, near, far, forward, act_two, slope_one, slope_two, *scratch):
     src, mid = scratch[:3], scratch[3:]
     masks = edge_masks()
     frames, rows = act_two.shape[0], source.shape[1]
     for f in range(frames):
-        g = base + f
-        fill(src, f, [(above, g, 4, masks[0]), (source, g, rows, None), (below, g, 4, masks[1])])
+        fill(src, f, source, base + f, rows, *halos(near, far, at + 4 * f, 4, masks))
 
     def first(f, r, v):
         for i in range(2):
@@ -186,7 +217,7 @@
 
 def middle_body(base, outside, decode, spots, *refs):
     acts, refs = list(zip(refs, spots)), refs[len(spots) :]
-    cot, above, below, forward, backward, mix = refs[:6]
+    cot, near, far, forward, backward, mix = refs[:6]
     back_three, side = refs[6:8]
     three, four, seed, back = refs[8:11], refs[11:14], refs[14:17], refs[17:20]
     slope_three, slope_four = refs[20:22]
@@ -215,8 +246,8 @@
                 if 2 <= r < rows + 2:
                     slope_three[i, r - 2] = slope_of(x, cdf).astype(BF16)
     for f in range(frames):
-        g = base + f
-        fill(seed, f, [(above, g, 2, masks[0]), (cot, g, rows, None), (below, g, 2, masks[1])])
+        at = near.shape[0] - 2 * (cot.shape[0] - base - f)
+        fill(seed, f, cot, base + f, rows, *halos(near, far, at, 2, masks))
 
     def third(f, r, v):
         for i in range(2):
@@ -253,7 +284,7 @@
     four, (buf, sems) = scratch[:3], scratch[3:]
     rows = one.shape[1] - 2
     for f, ref in enumerate((one, two)):
-        fill(four, f, [(ref, 0, rows + 2, None)])
+        fill(four, f, ref, 0, rows + 2)
     for copy in decode_into(forward.at[3], four, 2, rows, buf, out, base, sems):
         copy.wait()
 
@@ -261,7 +292,7 @@
 def unmix_body(outside, spots, *refs):
     picked = list(zip(refs, spots))
     backs, slopes = picked[:4], picked[4:]
-    unmix, back_two, last, first = refs[6:]
+    unmix, back_two, near, far = refs[6:]
     rows, chan = back_two.shape[1:3]
     weights = unmix[...]
     if outside:
@@ -282,20 +313,18 @@
                 slope, f = slopes[i]
                 value = (x * slope[f, r].astype(F32)).astype(BF16)
                 back_two[i, r] = value
-                if r < 2:
-                    first[i, r] = value
-                if r >= rows - 2:
-                    last[i, r - rows + 2] = value
-
-
-def grad_body(base, spots, back_two, above, below, *refs):
+    for i in range(2):
+        take(back_two, i, 2, near, far, 2 * i)
+
+
+def grad_body(base, spots, back_two, near, far, *refs):
     slopes, backward = list(zip(refs, spots)), refs[2]
     out, refs = refs[-9], refs[-8:]
     src, mid, (buf, sems) = refs[:3], refs[3:6], refs[6:]
     masks = edge_masks()
     frames, rows = back_two.shape[:2]
     for f in range(frames):
-        fill(src, f, [(above, f, 2, masks[0]), (back_two, f, rows, None), (below, f, 2, masks[1])])
+        fill(src, f, back_two, f, rows, *halos(near, far, 2 * f, 2, masks))
 
     def first(f, r, v):
         for i in range(2):
@@ -320,26 +349,33 @@
 
     sems = pltpu.SemaphoreType.DMA((2, rows // 4))
 
-    last, first, cot_last, cot_first = call(
-        pack_body, (frames_in, cotangent), [HBM] * 2,
-        [arr(count, 4)] * 2 + [arr(count, 2)] * 2, [VMEM] * 4,
-        [pltpu.SemaphoreType.DMA((4,))], name="pack",
+    half = count - 2
+    late_edges, edges = 4 * 2, 4 * half + 2 * count
+
+    near, far = call(
+        functools.partial(pack_late_body, half), (frames_in,), [VMEM],
+        [arr(late_edges)] * 2, [VMEM] * 2,
     )
-    above = passed_along(last, "rows", 1)
-    below = passed_along(first, "rows", -1)
+    near_late, far_late = exchanged(near, far)
+    near, far = call(
+        functools.partial(pack_body, half), (frames_in, cotangent), [VMEM] * 2,
+        [arr(edges)] * 2, [VMEM] * 2,
+    )
+    near, far = exchanged(near, far)
+    kernels = [jnp.transpose(k, (1, 2, 0, 3)) for k in (conv_one, conv_two, conv_three, conv_four)]
     two, four = 2 * chan, 4 * chan
     forward, backward, mix, unmix = call(
-        prep_body, (conv_one, conv_two, conv_three, conv_four, temporal), [VMEM] * 5,
+        prep_body, (*kernels, temporal), [VMEM] * 5,
         [jax.ShapeDtypeStruct((4, two, 3 * four), BF16)] * 2
         + [jax.ShapeDtypeStruct((two, four), BF16)] * 2,
-        [VMEM] * 4, flops=unit // 4, name="prep",
+        [VMEM] * 4, flops=unit // 4,
     )
 
-    def encode(base, n):
+    def encode(base, n, at, near, far):
         return call(
-            functools.partial(encode_body, base), (frames_in, above, below, forward), [VMEM] * 4,
+            functools.partial(encode_body, base, at), (frames_in, near, far, forward), [VMEM] * 4,
             [arr(n, rows + 4), arr(n, rows + 2), arr(n, rows)], [VMEM] * 3,
-            [vm(n, rows + 8)] * 3 + [vm(n, rows + 6)] * 3, flops=3 * unit * n // 2, name=f"encode{base}",
+            [vm(n, rows + 8)] * 3 + [vm(n, rows + 6)] * 3, flops=3 * unit * n // 2,
         )
 
     def middle(base, n, acts, outside):
@@ -352,56 +388,53 @@
             scratch += [vm(n, rows), sems]
         return call(
             functools.partial(middle_body, base, outside, decode, spots),
-            acts + (cotangent, cot_above, cot_below, forward, backward, mix),
+            acts + (cotangent, near, far, forward, backward, mix),
             [VMEM] * (len(acts) + 6), [arr(n, rows), side], [VMEM, ANY if decode else VMEM], scratch,
-            flops=5 * unit * n // 2, name=f"middle{base}",
-        )
-
-    def unmixed(backs, slopes, outside, name):
+            flops=5 * unit * n // 2,
+        )
+
+    def unmixed(backs, slopes, outside):
         ins, spots = zip(*(backs + slopes))
         return call(
             functools.partial(unmix_body, outside, spots), ins + (unmix,), [VMEM] * 7,
-            [arr(2, rows), arr(2, 2), arr(2, 2)], [VMEM] * 3, flops=unit // 3, name=name,
-        )
-
-    def grad(base, back_two, above, below, slopes, whole):
+            [arr(2, rows), arr(4), arr(4)], [VMEM] * 3, flops=unit // 3,
+        )
+
+    def grad(base, back_two, near, far, slopes, whole):
         slopes, spots = zip(*slopes)
-        ins, specs = (back_two, above, below) + slopes + (backward,), [VMEM] * 6
+        ins, specs = (back_two, near, far) + slopes + (backward,), [VMEM] * 6
         if whole is not None:
             ins, specs = ins + (whole,), specs + [ANY]
         return call(
             functools.partial(grad_body, base, spots), ins, specs, arr(count, rows, dtype=F32), ANY,
             [vm(2, rows + 4)] * 3 + [vm(2, rows + 2)] * 3 + [vm(2, rows, dtype=F32), sems],
-            {} if whole is None else {6: 0}, flops=2 * unit, name=f"grad{base}",
-        )
-
-    act_3, slope_one_3, slope_two_3 = encode(3, 1)
+            {} if whole is None else {6: 0}, flops=2 * unit,
+        )
+
+    act_3, slope_one_3, slope_two_3 = encode(half + 1, 1, 4, near_late, far_late)
     before_1 = passed_along(act_3, "tm", 1)
-    act_2, slope_one_2, slope_two_2 = encode(2, 1)
+    act_2, slope_one_2, slope_two_2 = encode(half, 1, 0, near_late, far_late)
     before_2 = passed_along(act_2, "tm", 1)
-    cot_last, cot_first, act_2 = lax.optimization_barrier((cot_last, cot_first, act_2))
-    cot_above = passed_along(cot_last, "rows", 1)
-    cot_below = passed_along(cot_first, "rows", -1)
-    act, slope_one, slope_two = encode(0, 2)
+    act, slope_one, slope_two = encode(0, half, 0, near, far)
+    back_late, decoded = middle(half, 2, [(act, 0), (act, 1), (act_2, 0), (act_3, 0)], 0)
+    before_1, back_late = lax.optimization_barrier((before_1, back_late))
     back_1, act_four_1 = middle(1, 1, [(before_1, 0), (act, 0), (act, 1)], 1)
     after_1 = passed_along(back_1, "tm", -1)
     before_2, back_1 = lax.optimization_barrier((before_2, back_1))
     back_0, act_four_0 = middle(0, 1, [(before_2, 0), (before_1, 0), (act, 0)], 2)
     after_0 = passed_along(back_0, "tm", -1)
-    act_3, back_0 = lax.optimization_barrier((act_3, back_0))
-    back_late, decoded = middle(2, 2, [(act, 0), (act, 1), (act_2, 0), (act_3, 0)], 0)
     backs = [(back_0, 0), (back_1, 0), (back_late, 0), (back_late, 1), (after_0, 0), (after_1, 0)]
-    early, last, first = unmixed(backs[:4], [(slope_two, 0), (slope_two, 1)], 0, "unmix0")
-    early_above, early_below = passed_along(last, "rows", 1), passed_along(first, "rows", -1)
-    late, last, first = unmixed(backs[2:], [(slope_two_2, 0), (slope_two_3, 0)], 2, "unmix2")
-    late_above, late_below = passed_along(last, "rows", 1), passed_along(first, "rows", -1)
+    early, near, far = unmixed(backs[:4], [(slope_two, 0), (slope_two, 1)], 0)
+    early_near, early_far = exchanged(near, far)
+    late, near, far = unmixed(backs[2:], [(slope_two_2, 0), (slope_two_3, 0)], 2)
+    late_near, late_far = exchanged(near, far)
     decoded = call(
         functools.partial(decode_body, 0), (act_four_0, act_four_1, forward, decoded), [VMEM] * 3 + [ANY],
         arr(count, rows), ANY, [vm(2, rows + 2)] * 3 + [vm(2, rows), sems], {3: 0},
-        flops=unit, name="decode0",
+        flops=unit,
     )
-    grad_in = grad(0, early, early_above, early_below, [(slope_one, 0), (slope_one, 1)], None)
-    grad_in = grad(2, late, late_above, late_below, [(slope_one_2, 0), (slope_one_3, 0)], grad_in)
+    grad_in = grad(0, early, early_near, early_far, [(slope_one, 0), (slope_one, 1)], None)
+    grad_in = grad(half, late, late_near, late_far, [(slope_one_2, 0), (slope_one_3, 0)], grad_in)
     return decoded, grad_in
 
 

time: 57.3 us -> 51 us (0.89)
  starting transfers between devices: 22.8 us -> 13.5 us
  waiting for transfers between devices: 11.2 us -> 15.8 us
  Pallas kernels: 19.1 us -> 18.1 us
    ppermute x12 -> x4, starting transfers between devices: 22.8 us -> 5.91 us  [passed_along(): lax.ppermute(value, axis, [(source, (source + steps) % count) for source...]
    ppermute x0 -> x8, starting transfers between devices: none -> 7.55 us  [swapped(): return lax.ppermute(value, ('tm', 'rows'), pairs)]
    ppermute x12 -> x4, waiting for transfers between devices: 11.2 us -> 15.8 us  [passed_along(): lax.ppermute(value, axis, [(source, (source + steps) % count) for source...]
    pallas_call x13 -> x14, Pallas kernels: 19.1 us -> 18.1 us  [call(): pl.pallas_call(body, out_shape=outs, in_specs=in_specs, out_specs=out_spe...]
    unnamed x22 -> x18, local copies, waits for them, and re-layouts: 2.99 us -> 2.47 us
  transfers between devices with their start and end apart: 12 -> 12, of which waited for: 5 -> 4; matrix products, arithmetic and copies ran while one was open for 1% -> 0% of each run, Pallas kernels for 25% -> 28%
where the time goes in v2:
time: 51 us; the launch traced here: 50.8 us
  Pallas kernels  18.1 us (35%)
  waiting for transfers between devices  15.8 us (31%)
  starting transfers between devices  13.5 us (26%)
  local copies, waits for them, and re-layouts  2.47 us (5%)
  between operations  1 us (2%)
    pallas_call x14, Pallas kernels, call(): pl.pallas_call(body, out_shape=outs, in_specs=in_specs, out_specs=out_spe...  18.1 us
    ppermute x4, waiting for transfers between devices, passed_along(): lax.ppermute(value, axis, [(source, (source + steps) % count) for source...  15.8 us
    ppermute x8, starting transfers between devices, swapped(): return lax.ppermute(value, ('tm', 'rows'), pairs)  7.55 us
    ppermute x4, starting transfers between devices, passed_along(): lax.ppermute(value, axis, [(source, (source + steps) % count) for source...  5.91 us
    unnamed x18, local copies, waits for them, and re-layouts  2.47 us
  transfers between devices with their start and end apart: 12, of which 4 were waited for; matrix products, arithmetic and copies ran while one was open for 0% of the time, Pallas kernels for 28%

profile of v2, /device:TPU:0, one launch (start us, length us, event | category | flops | bytes accessed | tf_op | source)
XLA Modules:
  0.0 50.8 jit_solution(17452914983012116948)
XLA Ops:
  0.6 0.0 copy-start
  0.6 1.2 %copy-done = bf16[4,16,64,128]{3,2,1,0:T(8,128)(2,1)S(1)} copy-done((bf16[4,16,64,128]{3,2,1,0:T(8,128)(2,1)S(1)}, bf16[4,16,64,128]{3,2,1,0:T(8,128)(2,1)}, u32[]{:S(2)}) %copy-start) | copy-done | bytes 1048600
  1.9 0.6 %collective-permute-start = (bf16[8,64,128]{2,1,0:T(8,128)(2,1)S(1)}, bf16[8,64,128]{2,1,0:T(8,128)(2,1)S(1)}, u32[]{:S(2)}, u32[]{:S(2)}) collective-permute-start(bf16[8,64,128]{2,1,0:T(8,128)(2,1)S(1)} %get-tuple-element.35), channel_id=1, source_target_pairs={{0,1},{1,0},{2,3},{3,2},{4,5},{5,4},{6,7},{7,6},{8,9},{9,8},{10,11... | collective-permute-start | bytes 393224 | tf_op jit(solution)/shard_map/ppermute | solution.py:36
  2.4 2.6 %collective-permute-start.1 = (bf16[8,64,128]{2,1,0:T(8,128)(2,1)S(1)}, bf16[8,64,128]{2,1,0:T(8,128)(2,1)S(1)}, u32[]{:S(2)}, u32[]{:S(2)}) collective-permute-start(bf16[8,64,128]{2,1,0:T(8,128)(2,1)S(1)} %get-tuple-element.36), channel_id=1, source_target_pairs={{0,8},{1,2},{2,1},{3,4},{4,3},{5,6},{6,5},{7,15},{8,0},{9,10},{10,... | collective-permute-start | bytes 393224 | tf_op jit(solution)/shard_map/ppermute | solution.py:36
  5.0 1.2 %copy-done.2 = bf16[4,16,64,128]{3,2,1,0:T(8,128)(2,1)S(1)} copy-done((bf16[4,16,64,128]{3,2,1,0:T(8,128)(2,1)S(1)}, bf16[4,16,64,128]{3,2,1,0:T(8,128)(2,1)}, u32[]{:S(2)}) %copy-start.2) | copy-done | bytes 1048600
  6.2 0.0 copy-start.8
  6.2 0.1 shard_map.90
  6.3 0.3 collective-permute-start.4
  6.6 1.5 %collective-permute-start.5 = (bf16[16,64,128]{2,1,0:T(8,128)(2,1)S(1)}, bf16[16,64,128]{2,1,0:T(8,128)(2,1)S(1)}, u32[]{:S(2)}, u32[]{:S(2)}) collective-permute-start(bf16[16,64,128]{2,1,0:T(8,128)(2,1)S(1)} %get-tuple-element.41), channel_id=1, source_target_pairs={{0,8},{1,2},{2,1},{3,4},{4,3},{5,6},{6,5},{7,15},{8,0},{9,10},{10,... | collective-permute-start | bytes 786440 | tf_op jit(solution)/shard_map/ppermute | solution.py:36
  8.1 0.0 copy-done.4
  8.1 0.0 copy-done.5
  8.1 0.0 copy-done.6
  8.1 0.0 copy-done.7
  8.1 0.0 copy-done.8
  8.1 0.7 %shard_map.87 = (bf16[4,128,768]{2,1,0:T(8,128)(2,1)S(1)}, bf16[4,128,768]{2,1,0:T(8,128)(2,1)S(1)}, bf16[128,256]{1,0:T(8,128)(2,1)S(1)}, bf16[128,256]{1,0:T(8,128)(2,1)S(1)}) custom-call(bf16[3,3,64,64]{3,2,1,0:T(8,128)(2,1)S(1)} %bitcast.4, bf16[3,3,64,64]{3,2,1,0:T(8,128)(2,1)S(1)} %bitcast.5, bf16[3,3,64,64]{3,2,1,0:T(8,128)(2,1)S(1)} %bitcast.6, ...), custom_call_target="tpu_custom_call" | custom-call | flops 75497472 | bytes 1048576 | tf_op jit(solution)/shard_map/pallas_call | solution.py:48
  8.8 0.0 collective-permute-done.near
  8.8 0.0 collective-permute-done.1.far
  8.8 1.2 %shard_map.89 = (bf16[1,20,64,128]{3,2,1,0:T(8,128)(2,1)S(1)}, bf16[1,18,64,128]{3,2,1,0:T(8,128)(2,1)S(1)}, bf16[1,16,64,128]{3,2,1,0:T(8,128)(2,1)S(1)}) custom-call(bf16[4,16,64,128]{3,2,1,0:T(8,128)(2,1)S(1)} %copy-done.1, bf16[8,64,128]{2,1,0:T(8,128)(2,1)S(1)} %collective-permute-done.near, bf16[8,64,128]{2,1,0:T(8,128)(2,1)S(1)} %collective-permute-done.1.far, ...), custom_call_target="tpu_custom_call" | custom-call | flops 452984832 | bytes 1048576 | tf_op jit(solution)/shard_map/pallas_call | solution.py:48
  9.9 1.2 %collective-permute-start.3 = (bf16[1,20,64,128]{3,2,1,0:T(8,128)(2,1)S(1)}, bf16[1,20,64,128]{3,2,1,0:T(8,128)(2,1)S(1)}, u32[]{:S(2)}, u32[]{:S(2)}) collective-permute-start(bf16[1,20,64,128]{3,2,1,0:T(8,128)(2,1)S(1)} %get-tuple-element.39.refs_3_), channel_id=1, source_target_pairs={{0,8},{8,16},{16,24},{24,0},{1,9},{9,17},{17,25},{25,1},{2,10},{10... | collective-permute-start | bytes 983048 | tf_op jit(solution)/shard_map/ppermute | solution.py:24
  11.2 1.1 %shard_map.88 = (bf16[1,20,64,128]{3,2,1,0:T(8,128)(2,1)S(1)}, bf16[1,18,64,128]{3,2,1,0:T(8,128)(2,1)S(1)}, bf16[1,16,64,128]{3,2,1,0:T(8,128)(2,1)S(1)}) custom-call(bf16[4,16,64,128]{3,2,1,0:T(8,128)(2,1)S(1)} %copy-done.1, bf16[8,64,128]{2,1,0:T(8,128)(2,1)S(1)} %collective-permute-done.near, bf16[8,64,128]{2,1,0:T(8,128)(2,1)S(1)} %collective-permute-done.1.far, ...), custom_call_target="tpu_custom_call" | custom-call | flops 452984832 | bytes 1048576 | tf_op jit(solution)/shard_map/pallas_call | solution.py:48
  12.3 0.0 copy-start.3
  12.3 1.9 %collective-permute-start.2 = (bf16[1,20,64,128]{3,2,1,0:T(8,128)(2,1)S(1)}, bf16[1,20,64,128]{3,2,1,0:T(8,128)(2,1)S(1)}, u32[]{:S(2)}, u32[]{:S(2)}) collective-permute-start(bf16[1,20,64,128]{3,2,1,0:T(8,128)(2,1)S(1)} %get-tuple-element.38.refs_2_), channel_id=1, source_target_pairs={{0,8},{8,16},{16,24},{24,0},{1,9},{9,17},{17,25},{25,1},{2,10},{10... | collective-permute-start | bytes 983048 | tf_op jit(solution)/shard_map/ppermute | solution.py:24
  14.2 0.0 collective-permute-done.4.near.refs_5_.refs_4_
  14.2 0.0 collective-permute-done.5.far.refs_6_.refs_5_
  14.2 1.9 %shard_map.91 = (bf16[2,20,64,128]{3,2,1,0:T(8,128)(2,1)S(1)}, bf16[2,18,64,128]{3,2,1,0:T(8,128)(2,1)S(1)}, bf16[2,16,64,128]{3,2,1,0:T(8,128)(2,1)S(1)}) custom-call(bf16[4,16,64,128]{3,2,1,0:T(8,128)(2,1)S(1)} %copy-done.1, bf16[16,64,128]{2,1,0:T(8,128)(2,1)S(1)} %collective-permute-done.4.near.refs_5_.refs_4_, ...), custom_call_target="tpu_custom_call" | custom-call | flops 905969664 | bytes 1048576 | tf_op jit(solution)/shard_map/pallas_call | solution.py:48
  16.1 0.0 copy-done.3
  16.1 3.8 %shard_map.92 = (bf16[2,16,64,128]{3,2,1,0:T(8,128)(2,1)S(1)}, bf16[4,16,64,128]{3,2,1,0:T(8,128)(2,1)}) custom-call(bf16[2,20,64,128]{3,2,1,0:T(8,128)(2,1)S(1)} %get-tuple-element.42.refs_0_.refs_1_.refs_2_, bf16[2,20,64,128]{3,2,1,0:T(8,128)(2,1)S(1)} %get-tuple-element.42.refs_0_.refs_1_.refs_2_, bf16[1,20,64,128]{3,2,1,0:T(8,128)(2,1)S(1)} %get-tuple-element.38.refs_2_, ...), custom_call_target="tpu_custom_call" | custom-call | flops 1509949440 | bytes 1048576 | tf_op jit(solution)/shard_map/pallas_call | solution.py:48
  19.9 1.6 %collective-permute-done.3.refs_0_.refs_1_ = bf16[1,20,64,128]{3,2,1,0:T(8,128)(2,1)S(1)} collective-permute-done((bf16[1,20,64,128]{3,2,1,0:T(8,128)(2,1)S(1)}, bf16[1,20,64,128]{3,2,1,0:T(8,128)(2,1)S(1)}, u32[]{:S(2)}, u32[]{:S(2)}) %collective-permute-start.3) | collective-permute-done | bytes 327712 | tf_op jit(solution)/shard_map/ppermute | solution.py:24
  21.5 1.6 %shard_map.93 = (bf16[1,16,64,128]{3,2,1,0:T(8,128)(2,1)S(1)}, bf16[1,18,64,128]{3,2,1,0:T(8,128)(2,1)S(1)}) custom-call(bf16[1,20,64,128]{3,2,1,0:T(8,128)(2,1)S(1)} %collective-permute-done.3.refs_0_.refs_1_, bf16[2,20,64,128]{3,2,1,0:T(8,128)(2,1)S(1)} %get-tuple-element.42.refs_0_.refs_1_.refs_2_, ...), custom_call_target="tpu_custom_call" | custom-call | flops 754974720 | bytes 1048576 | tf_op jit(solution)/shard_map/pallas_call | solution.py:48
  23.0 4.9 %collective-permute-done.2.refs_0_ = bf16[1,20,64,128]{3,2,1,0:T(8,128)(2,1)S(1)} collective-permute-done((bf16[1,20,64,128]{3,2,1,0:T(8,128)(2,1)S(1)}, bf16[1,20,64,128]{3,2,1,0:T(8,128)(2,1)S(1)}, u32[]{:S(2)}, u32[]{:S(2)}) %collective-permute-start.2) | collective-permute-done | bytes 327712 | tf_op jit(solution)/shard_map/ppermute | solution.py:24
  27.9 1.6 %shard_map.94 = (bf16[1,16,64,128]{3,2,1,0:T(8,128)(2,1)S(1)}, bf16[1,18,64,128]{3,2,1,0:T(8,128)(2,1)S(1)}) custom-call(bf16[1,20,64,128]{3,2,1,0:T(8,128)(2,1)S(1)} %collective-permute-done.2.refs_0_, bf16[1,20,64,128]{3,2,1,0:T(8,128)(2,1)S(1)} %collective-permute-done.3.refs_0_.refs_1_, ...), custom_call_target="tpu_custom_call" | custom-call | flops 754974720 | bytes 1048576 | tf_op jit(solution)/shard_map/pallas_call | solution.py:48
  29.5 1.5 %collective-permute-start.6 = (bf16[1,16,64,128]{3,2,1,0:T(8,128)(2,1)S(1)}, bf16[1,16,64,128]{3,2,1,0:T(8,128)(2,1)S(1)}, u32[]{:S(2)}, u32[]{:S(2)}) collective-permute-start(bf16[1,16,64,128]{3,2,1,0:T(8,128)(2,1)S(1)} %get-tuple-element.53.refs_0_), channel_id=1, source_target_pairs={{0,24},{8,0},{16,8},{24,16},{1,25},{9,1},{17,9},{25,17},{2,26},{10... | collective-permute-start | bytes 786440 | tf_op jit(solution)/shard_map/ppermute | solution.py:24
  31.0 1.3 %collective-permute-start.7 = (bf16[1,16,64,128]{3,2,1,0:T(8,128)(2,1)S(1)}, bf16[1,16,64,128]{3,2,1,0:T(8,128)(2,1)S(1)}, u32[]{:S(2)}, u32[]{:S(2)}) collective-permute-start(bf16[1,16,64,128]{3,2,1,0:T(8,128)(2,1)S(1)} %get-tuple-element.62.refs_1_), channel_id=1, source_target_pairs={{0,24},{8,0},{16,8},{24,16},{1,25},{9,1},{17,9},{25,17},{2,26},{10... | collective-permute-start | bytes 786440 | tf_op jit(solution)/shard_map/ppermute | solution.py:24
  32.3 0.3 shard_map.97
  32.7 0.1 collective-permute-start.10
  32.8 0.8 %collective-permute-start.11 = (bf16[4,64,128]{2,1,0:T(8,128)(2,1)S(1)}, bf16[4,64,128]{2,1,0:T(8,128)(2,1)S(1)}, u32[]{:S(2)}, u32[]{:S(2)}) collective-permute-start(bf16[4,64,128]{2,1,0:T(8,128)(2,1)S(1)} %get-tuple-element.66), channel_id=1, source_target_pairs={{0,8},{1,2},{2,1},{3,4},{4,3},{5,6},{6,5},{7,15},{8,0},{9,10},{10,... | collective-permute-start | bytes 196616 | tf_op jit(solution)/shard_map/ppermute | solution.py:36
  33.6 5.2 %collective-permute-done.6.refs_2_ = bf16[1,16,64,128]{3,2,1,0:T(8,128)(2,1)S(1)} collective-permute-done((bf16[1,16,64,128]{3,2,1,0:T(8,128)(2,1)S(1)}, bf16[1,16,64,128]{3,2,1,0:T(8,128)(2,1)S(1)}, u32[]{:S(2)}, u32[]{:S(2)}) %collective-permute-start.6) | collective-permute-done | bytes 262176 | tf_op jit(solution)/shard_map/ppermute | solution.py:24
  38.7 4.2 %collective-permute-done.7.refs_3_ = bf16[1,16,64,128]{3,2,1,0:T(8,128)(2,1)S(1)} collective-permute-done((bf16[1,16,64,128]{3,2,1,0:T(8,128)(2,1)S(1)}, bf16[1,16,64,128]{3,2,1,0:T(8,128)(2,1)S(1)}, u32[]{:S(2)}, u32[]{:S(2)}) %collective-permute-start.7) | collective-permute-done | bytes 262176 | tf_op jit(solution)/shard_map/ppermute | solution.py:24
  42.9 0.3 shard_map.96
  43.3 0.1 collective-permute-start.8
  43.3 1.8 %collective-permute-start.9 = (bf16[4,64,128]{2,1,0:T(8,128)(2,1)S(1)}, bf16[4,64,128]{2,1,0:T(8,128)(2,1)S(1)}, u32[]{:S(2)}, u32[]{:S(2)}) collective-permute-start(bf16[4,64,128]{2,1,0:T(8,128)(2,1)S(1)} %get-tuple-element.59), channel_id=1, source_target_pairs={{0,8},{1,2},{2,1},{3,4},{4,3},{5,6},{6,5},{7,15},{8,0},{9,10},{10,... | collective-permute-start | bytes 196616 | tf_op jit(solution)/shard_map/ppermute | solution.py:36
  45.1 1.4 %shard_map.95 = bf16[4,16,64,128]{3,2,1,0:T(8,128)(2,1)} custom-call(bf16[1,18,64,128]{3,2,1,0:T(8,128)(2,1)S(1)} %get-tuple-element.49.one, bf16[1,18,64,128]{3,2,1,0:T(8,128)(2,1)S(1)} %get-tuple-element.50.two, bf16[4,128,768]{2,1,0:T(8,128)(2,1)S(1)} %get-tuple-element.37.forward.refs_7_.refs_6_, ...), custom_call_target="tpu_custom_call", output_to_operand_aliasing={{}: (3, {})} | custom-call | flops 301989888 | bytes 1048576 | tf_op jit(solution)/shard_map/pallas_call | solution.py:48
  46.5 0.0 collective-permute-done.10.near
  46.5 0.0 collective-permute-done.11.far
  46.5 2.0 %shard_map.98.refs_3_ = f32[4,16,64,128]{3,2,1,0:T(8,128)} custom-call(bf16[2,16,64,128]{3,2,1,0:T(8,128)(2,1)S(1)} %get-tuple-element.64.back_two, bf16[4,64,128]{2,1,0:T(8,128)(2,1)S(1)} %collective-permute-done.10.near, bf16[4,64,128]{2,1,0:T(8,128)(2,1)S(1)} %collective-permute-done.11.far, ...), custom_call_target="tpu_custom_call" | custom-call | flops 603979776 | bytes 1048576 | tf_op jit(solution)/shard_map/pallas_call | solution.py:48
  48.6 0.0 collective-permute-done.8.near
  48.6 0.0 collective-permute-done.9.far
  48.6 2.0 %shard_map.99 = f32[4,16,64,128]{3,2,1,0:T(8,128)} custom-call(bf16[2,16,64,128]{3,2,1,0:T(8,128)(2,1)S(1)} %get-tuple-element.57.back_two, bf16[4,64,128]{2,1,0:T(8,128)(2,1)S(1)} %collective-permute-done.8.near, bf16[4,64,128]{2,1,0:T(8,128)(2,1)S(1)} %collective-permute-done.9.far, ...), custom_call_target="tpu_custom_call", output_to_operand_aliasing={{}: (6, {})} | custom-call | flops 603979776 | bytes 1048576 | tf_op jit(solution)/shard_map/pallas_call | solution.py:48
  (8 shorter events, 0.0 us)
Async XLA Ops:
  0.6 1.2 %copy-start = (bf16[4,16,64,128]{3,2,1,0:T(8,128)(2,1)S(1)}, bf16[4,16,64,128]{3,2,1,0:T(8,128)(2,1)}, u32[]{:S(2)}) copy-start(bf16[4,16,64,128]{3,2,1,0:T(8,128)(2,1)} %source.9) | copy-start | bytes 3145732
  1.9 6.9 %copy-start.1 = (bf16[4,16,64,128]{3,2,1,0:T(8,128)(2,1)S(1)}, bf16[4,16,64,128]{3,2,1,0:T(8,128)(2,1)}, u32[]{:S(2)}) copy-start(bf16[4,16,64,128]{3,2,1,0:T(8,128)(2,1)} %source.9) | copy-start | bytes 3145732
  1.9 6.9 %collective-permute-start = (bf16[8,64,128]{2,1,0:T(8,128)(2,1)S(1)}, bf16[8,64,128]{2,1,0:T(8,128)(2,1)S(1)}, u32[]{:S(2)}, u32[]{:S(2)}) collective-permute-start(bf16[8,64,128]{2,1,0:T(8,128)(2,1)S(1)} %get-tuple-element.35), channel_id=1, source_target_pairs={{0,1},{1,0},{2,3},{3,2},{4,5},{5,4},{6,7},{7,6},{8,9},{9,8},{10,11... | collective-permute-start | bytes 393224 | tf_op jit(solution)/shard_map/ppermute | solution.py:36
  2.4 6.3 %collective-permute-start.1 = (bf16[8,64,128]{2,1,0:T(8,128)(2,1)S(1)}, bf16[8,64,128]{2,1,0:T(8,128)(2,1)S(1)}, u32[]{:S(2)}, u32[]{:S(2)}) collective-permute-start(bf16[8,64,128]{2,1,0:T(8,128)(2,1)S(1)} %get-tuple-element.36), channel_id=1, source_target_pairs={{0,8},{1,2},{2,1},{3,4},{4,3},{5,6},{6,5},{7,15},{8,0},{9,10},{10,... | collective-permute-start | bytes 393224 | tf_op jit(solution)/shard_map/ppermute | solution.py:36
  5.0 1.2 %copy-start.2 = (bf16[4,16,64,128]{3,2,1,0:T(8,128)(2,1)S(1)}, bf16[4,16,64,128]{3,2,1,0:T(8,128)(2,1)}, u32[]{:S(2)}) copy-start(bf16[4,16,64,128]{3,2,1,0:T(8,128)(2,1)} %refs_3_.3) | copy-start | bytes 3145732
  6.2 1.8 %copy-start.4 = (bf16[64,3,3,64]{3,0,2,1:T(8,128)(2,1)S(1)}, bf16[64,3,3,64]{3,0,2,1:T(8,128)(2,1)}, u32[]{:S(2)}) copy-start(bf16[64,3,3,64]{3,0,2,1:T(8,128)(2,1)} %param.8) | copy-start | bytes 221188
  6.2 1.8 %copy-start.5 = (bf16[64,3,3,64]{3,0,2,1:T(8,128)(2,1)S(1)}, bf16[64,3,3,64]{3,0,2,1:T(8,128)(2,1)}, u32[]{:S(2)}) copy-start(bf16[64,3,3,64]{3,0,2,1:T(8,128)(2,1)} %param.9) | copy-start | bytes 221188
  6.2 1.8 %copy-start.6 = (bf16[64,3,3,64]{3,0,2,1:T(8,128)(2,1)S(1)}, bf16[64,3,3,64]{3,0,2,1:T(8,128)(2,1)}, u32[]{:S(2)}) copy-start(bf16[64,3,3,64]{3,0,2,1:T(8,128)(2,1)} %param.11) | copy-start | bytes 221188
  6.2 1.8 %copy-start.7 = (bf16[64,3,3,64]{3,0,2,1:T(8,128)(2,1)S(1)}, bf16[64,3,3,64]{3,0,2,1:T(8,128)(2,1)}, u32[]{:S(2)}) copy-start(bf16[64,3,3,64]{3,0,2,1:T(8,128)(2,1)} %param.12) | copy-start | bytes 221188
  6.2 1.8 %copy-start.8 = (bf16[3,64,64]{2,1,0:T(8,128)(2,1)S(1)}, bf16[3,64,64]{2,1,0:T(8,128)(2,1)}, u32[]{:S(2)}) copy-start(bf16[3,64,64]{2,1,0:T(8,128)(2,1)} %refs_4_.2) | copy-start | bytes 73732
  6.3 7.9 %collective-permute-start.4 = (bf16[16,64,128]{2,1,0:T(8,128)(2,1)S(1)}, bf16[16,64,128]{2,1,0:T(8,128)(2,1)S(1)}, u32[]{:S(2)}, u32[]{:S(2)}) collective-permute-start(bf16[16,64,128]{2,1,0:T(8,128)(2,1)S(1)} %get-tuple-element.40), channel_id=1, source_target_pairs={{0,1},{1,0},{2,3},{3,2},{4,5},{5,4},{6,7},{7,6},{8,9},{9,8},{10,11... | collective-permute-start | bytes 786440 | tf_op jit(solution)/shard_map/ppermute | solution.py:36
  6.6 7.6 %collective-permute-start.5 = (bf16[16,64,128]{2,1,0:T(8,128)(2,1)S(1)}, bf16[16,64,128]{2,1,0:T(8,128)(2,1)S(1)}, u32[]{:S(2)}, u32[]{:S(2)}) collective-permute-start(bf16[16,64,128]{2,1,0:T(8,128)(2,1)S(1)} %get-tuple-element.41), channel_id=1, source_target_pairs={{0,8},{1,2},{2,1},{3,4},{4,3},{5,6},{6,5},{7,15},{8,0},{9,10},{10,... | collective-permute-start | bytes 786440 | tf_op jit(solution)/shard_map/ppermute | solution.py:36
  9.9 11.5 %collective-permute-start.3 = (bf16[1,20,64,128]{3,2,1,0:T(8,128)(2,1)S(1)}, bf16[1,20,64,128]{3,2,1,0:T(8,128)(2,1)S(1)}, u32[]{:S(2)}, u32[]{:S(2)}) collective-permute-start(bf16[1,20,64,128]{3,2,1,0:T(8,128)(2,1)S(1)} %get-tuple-element.39.refs_3_), channel_id=1, source_target_pairs={{0,8},{8,16},{16,24},{24,0},{1,9},{9,17},{17,25},{25,1},{2,10},{10... | collective-permute-start | bytes 983048 | tf_op jit(solution)/shard_map/ppermute | solution.py:24
  12.3 3.8 %copy-start.3 = (bf16[4,16,64,128]{3,2,1,0:T(8,128)(2,1)S(1)}, bf16[4,16,64,128]{3,2,1,0:T(8,128)(2,1)}, u32[]{:S(2)}) copy-start(bf16[4,16,64,128]{3,2,1,0:T(8,128)(2,1)} %refs_3_.3) | copy-start | bytes 3145732
  12.3 15.6 %collective-permute-start.2 = (bf16[1,20,64,128]{3,2,1,0:T(8,128)(2,1)S(1)}, bf16[1,20,64,128]{3,2,1,0:T(8,128)(2,1)S(1)}, u32[]{:S(2)}, u32[]{:S(2)}) collective-permute-start(bf16[1,20,64,128]{3,2,1,0:T(8,128)(2,1)S(1)} %get-tuple-element.38.refs_2_), channel_id=1, source_target_pairs={{0,8},{8,16},{16,24},{24,0},{1,9},{9,17},{17,25},{25,1},{2,10},{10... | collective-permute-start | bytes 983048 | tf_op jit(solution)/shard_map/ppermute | solution.py:24
  29.5 9.2 %collective-permute-start.6 = (bf16[1,16,64,128]{3,2,1,0:T(8,128)(2,1)S(1)}, bf16[1,16,64,128]{3,2,1,0:T(8,128)(2,1)S(1)}, u32[]{:S(2)}, u32[]{:S(2)}) collective-permute-start(bf16[1,16,64,128]{3,2,1,0:T(8,128)(2,1)S(1)} %get-tuple-element.53.refs_0_), channel_id=1, source_target_pairs={{0,24},{8,0},{16,8},{24,16},{1,25},{9,1},{17,9},{25,17},{2,26},{10... | collective-permute-start | bytes 786440 | tf_op jit(solution)/shard_map/ppermute | solution.py:24
  31.0 11.9 %collective-permute-start.7 = (bf16[1,16,64,128]{3,2,1,0:T(8,128)(2,1)S(1)}, bf16[1,16,64,128]{3,2,1,0:T(8,128)(2,1)S(1)}, u32[]{:S(2)}, u32[]{:S(2)}) collective-permute-start(bf16[1,16,64,128]{3,2,1,0:T(8,128)(2,1)S(1)} %get-tuple-element.62.refs_1_), channel_id=1, source_target_pairs={{0,24},{8,0},{16,8},{24,16},{1,25},{9,1},{17,9},{25,17},{2,26},{10... | collective-permute-start | bytes 786440 | tf_op jit(solution)/shard_map/ppermute | solution.py:24
  32.7 13.8 %collective-permute-start.10 = (bf16[4,64,128]{2,1,0:T(8,128)(2,1)S(1)}, bf16[4,64,128]{2,1,0:T(8,128)(2,1)S(1)}, u32[]{:S(2)}, u32[]{:S(2)}) collective-permute-start(bf16[4,64,128]{2,1,0:T(8,128)(2,1)S(1)} %get-tuple-element.65), channel_id=1, source_target_pairs={{0,1},{1,0},{2,3},{3,2},{4,5},{5,4},{6,7},{7,6},{8,9},{9,8},{10,11... | collective-permute-start | bytes 196616 | tf_op jit(solution)/shard_map/ppermute | solution.py:36
  32.8 13.8 %collective-permute-start.11 = (bf16[4,64,128]{2,1,0:T(8,128)(2,1)S(1)}, bf16[4,64,128]{2,1,0:T(8,128)(2,1)S(1)}, u32[]{:S(2)}, u32[]{:S(2)}) collective-permute-start(bf16[4,64,128]{2,1,0:T(8,128)(2,1)S(1)} %get-tuple-element.66), channel_id=1, source_target_pairs={{0,8},{1,2},{2,1},{3,4},{4,3},{5,6},{6,5},{7,15},{8,0},{9,10},{10,... | collective-permute-start | bytes 196616 | tf_op jit(solution)/shard_map/ppermute | solution.py:36
  43.3 5.3 %collective-permute-start.8 = (bf16[4,64,128]{2,1,0:T(8,128)(2,1)S(1)}, bf16[4,64,128]{2,1,0:T(8,128)(2,1)S(1)}, u32[]{:S(2)}, u32[]{:S(2)}) collective-permute-start(bf16[4,64,128]{2,1,0:T(8,128)(2,1)S(1)} %get-tuple-element.58), channel_id=1, source_target_pairs={{0,1},{1,0},{2,3},{3,2},{4,5},{5,4},{6,7},{7,6},{8,9},{9,8},{10,11... | collective-permute-start | bytes 196616 | tf_op jit(solution)/shard_map/ppermute | solution.py:36
  43.3 5.3 %collective-permute-start.9 = (bf16[4,64,128]{2,1,0:T(8,128)(2,1)S(1)}, bf16[4,64,128]{2,1,0:T(8,128)(2,1)S(1)}, u32[]{:S(2)}, u32[]{:S(2)}) collective-permute-start(bf16[4,64,128]{2,1,0:T(8,128)(2,1)S(1)} %get-tuple-element.59), channel_id=1, source_target_pairs={{0,8},{1,2},{2,1},{3,4},{4,3},{5,6},{6,5},{7,15},{8,0},{9,10},{10,... | collective-permute-start | bytes 196616 | tf_op jit(solution)/shard_map/ppermute | solution.py:36
